TPU v7x, 32 devices: a whole 2x2x4 slice. The times are simulated.
32 devices in a mesh: dp: 32 (over z, y, x, core).
Axes of the slice: x: 2, y: 2, z: 4, core: 2. Of those that a mesh axis runs over, the one named last changes fastest.
Arguments:
- tokens_in: bfloat16 [16384, 1024], P('dp')
- w_one: bfloat16 [1024, 4096], replicated
- w_two: bfloat16 [4096, 1024], replicated
- item_table: bfloat16 [131072, 1024], P('dp')
- cand_ids: int32 [4096], replicated
- cand_logq: float32 [4096], replicated
- targets: int32 [16384], P('dp')
Outputs:
- output 1: float32 [], replicated
- output 2: float32 [131072, 1024], P('dp')
- output 3: float32 [1024, 4096], replicated
- output 4: float32 [4096, 1024], replicated
All inputs are finite; a program needn't handle non-finite values.
Results may differ from a plain program's by a relative error of at most 0.00824958.
Values are sent between devices in bfloat16 or wider.
A program may use at most 1 GiB of HBM per device.

v0:
```python
import jax
import jax.numpy as jnp
from jax import lax
from jax.sharding import PartitionSpec as P


def solution(mesh):
    dev_count = mesh.shape['dp']

    def local_step(x_blk, w_one, w_two, table_blk, cand_ids, cand_logq, y_blk):
        tok_dev = x_blk.shape[0]
        rows_dev = table_blk.shape[0]
        emb_dim = table_blk.shape[1]
        total_tok = tok_dev * dev_count
        row_base = lax.axis_index('dp') * rows_dev
        pre_act = jnp.dot(x_blk, w_one, preferred_element_type=jnp.float32).astype(jnp.bfloat16)
        act_val, gelu_back = jax.vjp(jax.nn.gelu, pre_act.astype(jnp.float32))
        hidden_act = act_val.astype(jnp.bfloat16)
        query_vec = jnp.dot(hidden_act, w_two, preferred_element_type=jnp.float32).astype(jnp.bfloat16)
        cand_local = cand_ids - row_base
        cand_owned = (cand_local >= 0) & (cand_local < rows_dev)
        cand_part = jnp.where(cand_owned[:, None],
                              jnp.take(table_blk, jnp.clip(cand_local, 0, rows_dev - 1), axis=0), 0)
        cand_rows = lax.psum(cand_part, 'dp')
        all_targets = lax.all_gather(y_blk, 'dp', tiled=True)
        tgt_local = all_targets - row_base
        tgt_owned = (tgt_local >= 0) & (tgt_local < rows_dev)
        tgt_part = jnp.where(tgt_owned[:, None],
                             jnp.take(table_blk, jnp.clip(tgt_local, 0, rows_dev - 1), axis=0), 0)
        tgt_rows = lax.psum_scatter(tgt_part, 'dp', scatter_dimension=0, tiled=True)
        z_tgt = jnp.einsum('td,td->t', query_vec, tgt_rows, preferred_element_type=jnp.float32)
        z_cand = jnp.einsum('td,sd->ts', query_vec, cand_rows, preferred_element_type=jnp.float32) - cand_logq[None, :]
        z_cand = jnp.where(y_blk[:, None] == cand_ids[None, :], -1e9, z_cand)
        peak_val = jnp.maximum(jnp.max(z_cand, axis=1), z_tgt)
        exp_total = jnp.exp(z_tgt - peak_val) + jnp.sum(jnp.exp(z_cand - peak_val[:, None]), axis=1)
        log_norm = peak_val + jnp.log(exp_total)
        loss_val = lax.psum(jnp.sum(log_norm - z_tgt), 'dp') / total_tok
        dz_tgt = (jnp.exp(z_tgt - log_norm) - 1.0) / total_tok
        dz_cand = (jnp.exp(z_cand - log_norm[:, None]) / total_tok).astype(jnp.bfloat16)
        d_query = (dz_tgt[:, None] * tgt_rows.astype(jnp.float32)
                   + jnp.dot(dz_cand, cand_rows, preferred_element_type=jnp.float32)).astype(jnp.bfloat16)
        cand_grad = lax.psum(jnp.einsum('ts,td->sd', dz_cand, query_vec, preferred_element_type=jnp.float32), 'dp')
        grad_two = lax.psum(jnp.einsum('tf,td->fd', hidden_act, d_query, preferred_element_type=jnp.float32), 'dp')
        d_act = jnp.einsum('td,fd->tf', d_query, w_two, preferred_element_type=jnp.float32)
        d_pre = gelu_back(d_act.astype(jnp.bfloat16).astype(jnp.float32))[0].astype(jnp.bfloat16)
        grad_one = lax.psum(jnp.einsum('ti,tf->if', x_blk, d_pre, preferred_element_type=jnp.float32), 'dp')
        query_all = lax.all_gather(query_vec, 'dp', tiled=True)
        dz_all = lax.all_gather(dz_tgt, 'dp', tiled=True)
        cand_slot = jnp.where(cand_owned, cand_local, rows_dev)
        tgt_slot = jnp.where(tgt_owned, tgt_local, rows_dev)
        grad_table = jnp.zeros((rows_dev, emb_dim), jnp.float32)
        grad_table = grad_table.at[cand_slot].add(cand_grad, mode='drop')
        grad_table = grad_table.at[tgt_slot].add(dz_all[:, None] * query_all.astype(jnp.float32), mode='drop')
        return loss_val, grad_table, grad_one, grad_two

    return jax.shard_map(local_step, mesh=mesh,
                         in_specs=(P('dp', None), P(), P(), P('dp', None), P(), P(), P('dp')),
                         out_specs=(P(), P('dp', None), P(), P()), check_vma=False)
```

profile of v0, /device:TPU:0, one launch (start us, length us, event | category | flops | bytes accessed | tf_op | source)
XLA Modules:
  0.0 1847.7 jit_solution(16220055963955288325)
XLA Ops:
  7.2 43.6 %all-gather = s32[32,1,512]{2,1,0:T(1,128)S(1)} all-gather(s32[1,1,512]{2,1,0:T(1,128)} %bitcast.24), channel_id=1, replica_groups=mesh['dp'=32] {'dp'}, dimensions={0}, use_global_device_ids=true | all-gather | bytes 67584 | tf_op jit(solution)/shard_map/all_gather | solution.py:25
  50.8 0.7 compare_select_fusion
  51.5 84.7 %gather_fusion.1 = bf16[16384,1024]{1,0:T(8,128)(2,1)} fusion(bf16[4096,1024]{1,0:T(8,128)(2,1)} %param.10, s32[16384]{0:T(1024)S(1)} %get-tuple-element.22), kind=kCustom, calls=%fused_computation.1 | custom fusion | bytes 67174400 | tf_op jit(solution)/shard_map/jit(_take)/gather | solution.py:29
  136.3 22.7 %select_select_fusion = bf16[16384,1024]{1,0:T(8,128)(2,1)} fusion(bf16[16384,1024]{1,0:T(8,128)(2,1)} %gather_fusion.1, pred[16384]{0:T(1024)(128)(4,1)S(1)} %get-tuple-element.24, pred[16384]{0:T(1024)(128)(4,1)S(1)} %get-tuple-element.23), kind=kLoop, calls=%fused_computation.8 | loop fusion | flops 33554432 | bytes 67141632 | tf_op jit(solution)/shard_map/jit(_where)/select_n | solution.py:28
  160.3 25.2 %gather_fusion = bf16[4096,1024]{1,0:T(8,128)(2,1)} fusion(bf16[4096,1024]{1,0:T(8,128)(2,1)} %param.10, s32[4096]{0:T(1024)S(1)} %get-tuple-element.26), kind=kCustom, calls=%fused_computation | custom fusion | bytes 16793600 | tf_op jit(solution)/shard_map/jit(_take)/gather | solution.py:23
  185.5 7.5 select_select_fusion.1
  193.4 9.4 convolution_convert_fusion.1
  202.8 306.8 %reduce-scatter.2.cloned.1.call-done = bf16[512,1024]{1,0:T(8,128)(2,1)} async-done(((bf16[16384,1024]{1,0:T(8,128)(2,1)}), bf16[512,1024]{1,0:T(8,128)(2,1)}) %reduce-scatter.2.cloned.1.call-update) | async-done | bytes 1048592 | tf_op jit(solution)/shard_map/reduce_scatter | solution.py:30
  509.6 10.2 fusion.24
  519.9 182.1 %all-reduce.4.cloned.1.call-done = bf16[4096,1024]{1,0:T(8,128)(2,1)} async-done(((bf16[4096,1024]{1,0:T(8,128)(2,1)}), bf16[4096,1024]{1,0:T(8,128)(2,1)}) %all-reduce.4.cloned.1.call-update) | async-done | bytes 8388624 | tf_op jit(solution)/shard_map/psum | solution.py:24
  701.9 7.3 fusion.39
  709.3 1.3 exponential_reduce_fusion
  710.6 9.2 fusion.38
  719.9 4.6 fusion.26
  724.5 17.7 convolution_bitcast_fusion
  742.3 14.2 fusion.35
  757.7 41.6 %psum.36 = f32[]{:T(128)} all-reduce(f32[]{:T(128)} %subtract_reduce_fusion), channel_id=1, replica_groups=mesh['dp'=32] {'dp'}, use_global_device_ids=true, to_apply=%region_5.6 | all-reduce | flops 1 | bytes 8 | tf_op jit(solution)/shard_map/psum | solution.py:37
  799.9 41.1 %all-gather.1 = f32[32,1,512]{2,1,0:T(1,128)S(1)} all-gather(f32[1,1,512]{2,1,0:T(1,128)S(1)} %bitcast.23), channel_id=1, replica_groups=mesh['dp'=32] {'dp'}, dimensions={0}, use_global_device_ids=true | all-gather | bytes 67584 | tf_op jit(solution)/shard_map/all_gather | solution.py:48
  841.0 638.7 %all-reduce.6.cloned.1.call-done = (f32[4096,1024]{1,0:T(8,128)}, f32[1024,4096]{0,1:T(8,128)}, f32[4096,1024]{1,0:T(8,128)}) async-done(((f32[4096,1024]{1,0:T(8,128)}, f32[1024,4096]{0,1:T(8,128)}, f32[4096,1024]{1,0:T(8,128)}), (f32[4096,1024]{1,0:T(8,128)}, f32[1024,4096]{0,1:T(8,128)}, f32[4096,1024]{1,0:T(8,128)})) %all-reduce.6.cloned.1.call-update) | async-done | bytes 50331664 | tf_op jit(solution)/shard_map/psum | solution.py:42
  1479.7 17.4 copy.13
  1497.1 43.5 %scatter_custom_fusion = f32[4096,1024]{1,0:T(8,128)} fusion(s32[4096]{0:T(1024)} %get-tuple-element.25, f32[4096,1024]{1,0:T(8,128)} %get-tuple-element.16, f32[]{:T(128)} %constant.37.clone.1), kind=kCustom, calls=%fused_computation.28 | custom fusion | flops 4194304 | bytes 16777728 | tf_op jit(solution)/shard_map/scatter-add | solution.py:52
  1540.6 135.0 %all-gather.4.cloned.1.call-done = bf16[16384,1024]{1,0:T(8,128)(2,1)} async-done(((bf16[512,1024]{1,0:T(8,128)(2,1)}), bf16[16384,1024]{1,0:T(8,128)(2,1)}) %all-gather.4.cloned.1.call-update) | async-done | bytes 33554448 | tf_op jit(solution)/shard_map/all_gather | solution.py:47
  1675.6 152.2 %scatter_custom_fusion.1 = f32[4096,1024]{1,0:T(8,128)} fusion(f32[4096,1024]{1,0:T(8,128)} %scatter_custom_fusion, s32[16384]{0:T(1024)} %get-tuple-element.21, bf16[16384,1024]{1,0:T(8,128)(2,1)} %all-gather.4.cloned.1.call-done, f32[16384]{0:T(1024)S(1)} %bitcast.21), kind=kCustom, calls=%fused_computation.4 | custom fusion | flops 50331648 | bytes 50397184 | tf_op jit(solution)/shard_map/scatter-add | solution.py:53
  1827.8 12.0 copy.24
  (32 shorter events, 3.0 us)
Async XLA Ops:
  7.2 186.3 %copy-start = (bf16[512,1024]{1,0:T(8,128)(2,1)S(1)}, bf16[512,1024]{1,0:T(8,128)(2,1)}, u32[]{:S(2)}) copy-start(bf16[512,1024]{1,0:T(8,128)(2,1)} %param.7) | copy-start | bytes 3145732
  7.2 502.4 %reduce-scatter.2.cloned.1.call-start = ((), (), s32[]{:S(2)}) async-start(), calls=%async_computation.2 | async-start | bytes 34603008 | tf_op jit(solution)/shard_map/reduce_scatter | solution.py:30
  158.9 0.7 copy-start.2
  159.0 543.0 %all-reduce.4.cloned.1.call-start = ((), (), s32[]{:S(2)}) async-start(), calls=%async_computation.1 | async-start | bytes 16777216 | tf_op jit(solution)/shard_map/psum | solution.py:24
  193.1 1286.6 %all-reduce.6.cloned.1.call-start = ((), (), s32[]{:S(2)}) async-start(), calls=%async_computation.4 | async-start | bytes 100663296 | tf_op jit(solution)/shard_map/psum | solution.py:42
  202.8 499.1 %copy-start.3 = (s32[512]{0:T(512)S(1)}, s32[512]{0:T(512)}, u32[]{:S(2)}) copy-start(s32[512]{0:T(512)} %param.13) | copy-start | bytes 6148
  202.8 499.1 %copy-start.5 = (f32[4096]{0:T(1024)S(1)}, f32[4096]{0:T(1024)}, u32[]{:S(2)}) copy-start(f32[4096]{0:T(1024)} %param.12) | copy-start | bytes 49156
  519.9 190.7 %copy-start.1 = (bf16[512,1024]{1,0:T(8,128)(2,1)}, bf16[512,1024]{1,0:T(8,128)(2,1)S(1)}, u32[]{:S(2)}) copy-start(bf16[512,1024]{1,0:T(8,128)(2,1)S(1)} %get-tuple-element.30) | copy-start | bytes 3145732
  709.3 10.6 slice-start
  710.6 9.3 slice-start.1
  710.6 9.3 copy-start.4
  756.5 919.2 %all-gather.4.cloned.1.call-start = ((), (), s32[]{:S(2)}) async-start(), calls=%async_computation.3 | async-start | bytes 34603008 | tf_op jit(solution)/shard_map/all_gather | solution.py:47
Sparse Core Ops, SparseCore 0:
  159.1 350.4 reduce-scatter.1
  515.9 186.0 all-reduce.3
  756.6 723.0 all-reduce.5
  1482.4 193.1 all-gather.3
where the time goes:
time: 1850 us
  waiting for transfers between devices  1260 us (68%)
  other arithmetic  229 us (12%)
  local copies, waits for them, and re-layouts  140 us (8%)
  blocking collectives  126 us (7%)
  matrix products  72.8 us (4%)
    psum x1, waiting for transfers between devices, local_step(): lax.psum(jnp.einsum('ts,td->sd', dz_cand, query_vec, preferred_element_ty...  639 us
    reduce_scatter x1, waiting for transfers between devices, local_step(): tgt_rows = lax.psum_scatter(tgt_part, 'dp', scatter_dimension=0, tiled=True)  307 us
    psum x1, waiting for transfers between devices, local_step(): cand_rows = lax.psum(cand_part, 'dp')  182 us
    scatter-add x1, other arithmetic, local_step(): grad_table.at[tgt_slot]  152 us
    all_gather x1, waiting for transfers between devices, local_step(): query_all = lax.all_gather(query_vec, 'dp', tiled=True)  135 us
    gather x1, local copies, waits for them, and re-layouts, local_step(): jnp.take(table_blk, jnp.clip(tgt_local, 0, rows_dev - 1), axis=0)  84.7 us
    all_gather x1, blocking collectives, local_step(): all_targets = lax.all_gather(y_blk, 'dp', tiled=True)  43.6 us
    scatter-add x1, other arithmetic, local_step(): grad_table = grad_table.at[cand_slot].add(cand_grad, mode='drop')  43.5 us
  transfers between devices with their start and end apart: 4, of which 4 were waited for; matrix products, arithmetic and copies ran while one was open for 6% of the time, Pallas kernels for 0%

commit v1 on v0

v1 whole, which is shorter than its diff:
```python
import functools

import jax
import jax.numpy as jnp
from jax import lax
from jax.experimental import pallas as pl
from jax.experimental.pallas import tpu as pltpu
from jax.sharding import PartitionSpec as P

MESH = pl.DeviceIdType.MESH
PARTS = 8


def spread_kernel(n, in_ref, out_ref, send_sem, recv_sem):
    me = lax.axis_index('dp')
    barrier = pltpu.get_barrier_semaphore()

    def greet(i, carry):
        pl.semaphore_signal(barrier, inc=1, device_id=(lax.rem(me + i, n),), device_id_type=MESH)
        return carry

    lax.fori_loop(1, n, greet, 0)
    pl.semaphore_wait(barrier, n - 1)

    def send(i, carry):
        pltpu.make_async_remote_copy(
            src_ref=in_ref, dst_ref=out_ref.at[me], send_sem=send_sem, recv_sem=recv_sem,
            device_id=(lax.rem(me + i, n),), device_id_type=MESH).start()
        return carry

    lax.fori_loop(1, n, send, 0)
    others = out_ref.at[pl.ds(0, n - 1)]
    drain = pltpu.make_async_remote_copy(
        src_ref=others, dst_ref=others, send_sem=send_sem, recv_sem=recv_sem,
        device_id=(me,), device_id_type=MESH)
    drain.wait_recv()
    drain.wait_send()
    out_ref[me] = in_ref[...]


def spread(block, n, cid):
    return pl.pallas_call(
        functools.partial(spread_kernel, n),
        out_shape=jax.ShapeDtypeStruct((n,) + block.shape, block.dtype),
        in_specs=[pl.BlockSpec(memory_space=pltpu.VMEM)],
        out_specs=pl.BlockSpec(memory_space=pltpu.VMEM),
        scratch_shapes=[pltpu.SemaphoreType.DMA, pltpu.SemaphoreType.DMA],
        compiler_params=pltpu.CompilerParams(collective_id=cid, has_side_effects=True),
        name=f'spread_{cid}',
    )(block)


def reduce_kernel(tile, steps, in_ref, out_ref, acc, *scratch):
    got, (load_sem, send_sem, recv_sem, store_sem) = scratch[:steps], scratch[steps:]
    me = lax.axis_index('dp')
    core = lax.rem(me, 2)
    xb, yb = lax.rem(me // 2, 2), lax.rem(me // 4, 2)
    z0, z1 = lax.rem(me // 8, 2), lax.rem(me // 16, 2)
    w1, w2 = 1 + core, 2 - core
    b1 = xb * (1 - core) + yb * core
    b2 = yb * (1 - core) + xb * core
    bits = (core, b1, b2, z0, z1)
    mates = [me + 2 * w * (1 - 2 * b) for b, w in zip(bits[1:], (w1, w2, 4, 8))]
    mates = ([me + 1 - 2 * core] + mates)[:steps]
    barrier = pltpu.get_barrier_semaphore()
    for mate in mates:
        pl.semaphore_signal(barrier, inc=1, device_id=(mate,), device_id_type=MESH)

    def piece(part):
        if tile[0] is None:
            return (slice(None), pl.ds(part * tile[1], tile[1]))
        return (pl.ds(part * tile[0], tile[0]),)

    def load(part):
        return pltpu.make_async_copy(in_ref.at[(slice(None), core) + piece(part)], acc.at[part], load_sem.at[part])

    for part in range(PARTS):
        load(part).start()
    pl.semaphore_wait(barrier, steps)

    def place(step, i, bit):
        if step == 1:
            return bit * w1 + lax.rem(i, 2) * w2 + (i // 2) * 4
        base = b1 * w1
        if step == 2:
            return base + bit * w2 + i * 4
        base = base + b2 * w2
        if step == 3:
            return base + bit * 4 + i * 8
        return base + z0 * 4 + bit * 8

    def send(step, part):
        if step == 0:
            pltpu.make_async_remote_copy(
                src_ref=in_ref.at[(slice(None), 1 - core) + piece(part)], dst_ref=got[0].at[part],
                send_sem=send_sem.at[0, part], recv_sem=recv_sem.at[0, part],
                device_id=(mates[0],), device_id_type=MESH).start()
            return

        def one(i, carry):
            pltpu.make_async_remote_copy(
                src_ref=acc.at[part, place(step, i, 1 - bits[step])], dst_ref=got[step].at[part, i],
                send_sem=send_sem.at[step, part], recv_sem=recv_sem.at[step, part],
                device_id=(mates[step],), device_id_type=MESH).start()
            return carry
        lax.fori_loop(0, got[step].shape[1], one, 0)

    def whole(step, part):
        return pltpu.make_async_remote_copy(
            src_ref=got[step].at[part], dst_ref=got[step].at[part],
            send_sem=send_sem.at[step, part], recv_sem=recv_sem.at[step, part],
            device_id=(mates[step],), device_id_type=MESH)

    def add(step, part):
        def one(i, carry):
            at = i if step == 0 else place(step, i, bits[step])
            acc[part, at] = acc[part, at] + got[step][part, i]
            return carry
        lax.fori_loop(0, got[step].shape[1], one, 0)

    def store(part):
        return pltpu.make_async_copy(acc.at[part, me // 2], out_ref.at[piece(part)], store_sem.at[part])

    for tick in range(PARTS + steps):
        for step in range(steps - 1, -1, -1):
            part = tick - 1 - step
            if 0 <= part < PARTS:
                if step == 0:
                    load(part).wait()
                whole(step, part).wait_recv()
                add(step, part)
                if step < steps - 1:
                    send(step + 1, part)
                else:
                    store(part).start()
        if tick < PARTS:
            send(0, tick)
    for part in range(PARTS):
        for step in range(steps):
            whole(step, part).wait_send()
        store(part).wait()


def reduce_scatter(x, n, cid):
    per, rest = x.shape[0] // n, x.shape[1:]
    if len(rest) == 2 or per // PARTS >= 8:
        tile, piece = (per // PARTS, None), (per // PARTS,) + rest
    else:
        tile, piece = (None, rest[0] // PARTS), (per, rest[0] // PARTS)
    steps = n.bit_length() - 1
    got = [pltpu.VMEM((PARTS, n >> (s + 1)) + piece, x.dtype) for s in range(steps)]
    size = x.size * x.dtype.itemsize
    return pl.pallas_call(
        functools.partial(reduce_kernel, tile, steps),
        out_shape=jax.ShapeDtypeStruct((per,) + rest, x.dtype),
        in_specs=[pl.BlockSpec(memory_space=pl.ANY)],
        out_specs=pl.BlockSpec(memory_space=pl.ANY),
        scratch_shapes=[pltpu.VMEM((PARTS, n // 2) + piece, x.dtype)] + got + [
            pltpu.SemaphoreType.DMA((PARTS,)),
            pltpu.SemaphoreType.DMA((steps, PARTS)),
            pltpu.SemaphoreType.DMA((steps, PARTS)),
            pltpu.SemaphoreType.DMA((PARTS,)),
        ],
        compiler_params=pltpu.CompilerParams(collective_id=cid, has_side_effects=True,
                                             vmem_limit_bytes=min(size * 3 // 2 + 4 * 2**20, 67043328)),
        name=f'reduce_{cid}',
    )(x.reshape((n // 2, 2, per) + rest))


SLOT_BITS = 1024
OUT_ROWS = 256


def pick_kernel(n, count, rows_dev, keys, first, last, table, rows_out, buf, sems):
    base = lax.axis_index('dp') * rows_dev

    def zero(i, carry):
        for slot in range(2):
            buf[slot, pl.ds(i * 32, 32)] = jnp.zeros((32,) + buf.shape[2:], buf.dtype)
        return carry

    lax.fori_loop(0, count // 32, zero, 0)

    def out_copy(j, slot):
        return pltpu.make_async_copy(buf.at[slot], rows_out.at[j], sems.at[slot])

    def per_dev(j, carry):
        slot = lax.rem(j, 2)

        @pl.when(j >= 2)
        def _():
            out_copy(j - 2, slot).wait()

            def clear(i, c):
                buf[slot, i] = jnp.zeros(buf.shape[2:], buf.dtype)
                return c

            lax.fori_loop(first[j - 2], last[j - 2], clear, 0)

        def one(i, c):
            buf[slot, i] = table[keys[j * count + i] // SLOT_BITS - base]
            return c

        lax.fori_loop(first[j], last[j], one, 0)
        out_copy(j, slot).start()
        return carry

    lax.fori_loop(0, n, per_dev, 0)
    out_copy(n - 2, 0).wait()
    out_copy(n - 1, 1).wait()


def pick_rows(table3, keys, first, last, n, count):
    smem = pl.BlockSpec(memory_space=pltpu.SMEM)
    return pl.pallas_call(
        functools.partial(pick_kernel, n, count, table3.shape[0]),
        out_shape=jax.ShapeDtypeStruct((n, count) + table3.shape[1:], table3.dtype),
        in_specs=[smem, smem, smem, pl.BlockSpec(memory_space=pltpu.VMEM)],
        out_specs=pl.BlockSpec(memory_space=pl.ANY),
        scratch_shapes=[pltpu.VMEM((2, count) + table3.shape[1:], table3.dtype), pltpu.SemaphoreType.DMA((2,))],
        compiler_params=pltpu.CompilerParams(vmem_limit_bytes=24 * 2**20),
        name='pick_rows',
    )(keys, first, last, table3)


def table_kernel(n, count, tok_dev, rows_dev, lane, keys, first, last, scale, query, cand, out_ref, acc):
    step = pl.program_id(0)
    base = lax.axis_index('dp') * rows_dev

    @pl.when(step == 0)
    def _():
        def zero(i, carry):
            acc[pl.ds(i * 64, 64)] = jnp.zeros((64,) + acc.shape[1:], jnp.float32)
            return carry

        lax.fori_loop(0, rows_dev // 64, zero, 0)

    @pl.when(step < n)
    def _():
        def one(i, carry):
            key = keys[step * count + i]
            at = key // SLOT_BITS - base
            slot = lax.rem(key, SLOT_BITS)

            @pl.when(slot < tok_dev)
            def _():
                acc[at] = acc[at] + scale[step * tok_dev + slot] * query[slot].astype(jnp.float32)

            @pl.when(slot >= tok_dev)
            def _():
                acc[at] = acc[at] + cand[slot - tok_dev]

            return carry

        lax.fori_loop(first[step], last[step], one, 0)

    @pl.when(step >= n)
    def _():
        for j in range(acc.shape[1]):
            out_ref[:, j * lane:(j + 1) * lane] = acc[pl.ds((step - n) * OUT_ROWS, OUT_ROWS), j, :]


def table_grad(keys, first, last, scale, query, cand, rows_dev, n, count):
    tok_dev, cand_dev = query.shape[0] // n, cand.shape[0] // n
    sub, lane = query.shape[1:]
    smem = pl.BlockSpec(memory_space=pltpu.SMEM)
    size = 4 * rows_dev * sub * lane
    return pl.pallas_call(
        functools.partial(table_kernel, n, count, tok_dev, rows_dev, lane),
        grid=(n + rows_dev // OUT_ROWS,),
        out_shape=jax.ShapeDtypeStruct((rows_dev, sub * lane), jnp.float32),
        in_specs=[smem, smem, smem, smem,
                  pl.BlockSpec((tok_dev, sub, lane), lambda i: (jnp.minimum(i, n - 1), 0, 0)),
                  pl.BlockSpec((cand_dev, sub, lane), lambda i: (jnp.minimum(i, n - 1), 0, 0))],
        out_specs=pl.BlockSpec((OUT_ROWS, sub * lane), lambda i: (jnp.maximum(i - n, 0), 0)),
        scratch_shapes=[pltpu.VMEM((rows_dev, sub, lane), jnp.float32)],
        cost_estimate=pl.CostEstimate(flops=30_000_000_000, bytes_accessed=4 * size, transcendentals=0),
        compiler_params=pltpu.CompilerParams(vmem_limit_bytes=size + 12 * 2**20),
        name='table_grad',
    )(keys, first, last, scale, query, cand)


def outer_kernel(left, right, out_ref):
    out_ref[...] = jnp.dot(left[...], right[...], preferred_element_type=jnp.float32)


def outer(left, right):
    rows, depth = left.shape
    cols = right.shape[1]
    high, wide = rows // 2, cols // 8
    return pl.pallas_call(
        outer_kernel,
        grid=(rows // high, cols // wide),
        out_shape=jax.ShapeDtypeStruct((rows, cols), jnp.float32),
        in_specs=[pl.BlockSpec((high, depth), lambda i, j: (i, 0)), pl.BlockSpec((depth, wide), lambda i, j: (0, j))],
        out_specs=pl.BlockSpec((high, wide), lambda i, j: (i, j)),
        cost_estimate=pl.CostEstimate(flops=2 * rows * cols * depth, bytes_accessed=4 * rows * cols, transcendentals=0),
        compiler_params=pltpu.CompilerParams(vmem_limit_bytes=16 * 2**20),
        name='outer',
    )(left, right)


def solution(mesh):
    n = mesh.shape['dp']

    def local_step(x_blk, w_one, w_two, table_blk, cand_ids, cand_logq, y_blk):
        tok_dev = x_blk.shape[0]
        rows_dev, emb_dim = table_blk.shape
        total_tok = tok_dev * n
        cand_dev = cand_ids.shape[0] // n
        count = tok_dev + cand_dev
        lane = 128
        sub = emb_dim // lane
        me = lax.axis_index('dp')

        slots = jnp.arange(count, dtype=jnp.int32)
        wants = jnp.concatenate([y_blk, lax.dynamic_slice(cand_ids, (me * cand_dev,), (cand_dev,))]) * SLOT_BITS + slots
        rank = jnp.sum((wants[None, :] < wants[:, None]).astype(jnp.int32), axis=1)
        sorted_own = jnp.sum(jnp.where(rank[:, None] == slots[None, :], wants[:, None], 0), axis=0)
        block = jnp.pad(sorted_own, (0, (-count) % (8 * lane))).reshape(-1, lane)
        everyone = spread(block, n, 0).reshape(n, -1)[:, :count]
        first = jnp.sum((everyone < me * rows_dev * SLOT_BITS).astype(jnp.int32), axis=1)
        last = jnp.sum((everyone - me * rows_dev * SLOT_BITS < rows_dev * SLOT_BITS).astype(jnp.int32), axis=1)
        keys = everyone.reshape(-1)

        picked = pick_rows(table_blk.reshape(rows_dev, sub, lane), keys, first, last, n, count)
        got = reduce_scatter(picked.reshape(n * count, sub, lane), n, 5).reshape(count, emb_dim)
        own_cand = got.at[rank[tok_dev:]].get(mode='promise_in_bounds')
        cand_rows = lax.all_gather(own_cand, 'dp', tiled=True)
        tgt_rows = got.at[rank[:tok_dev]].get(mode='promise_in_bounds')

        x_flip = lax.optimization_barrier(x_blk.T)
        pre_act = jnp.dot(x_blk, w_one, preferred_element_type=jnp.float32).astype(jnp.bfloat16)
        act_val, gelu_back = jax.vjp(jax.nn.gelu, pre_act.astype(jnp.float32))
        hidden_act = act_val.astype(jnp.bfloat16)
        query_vec = jnp.dot(hidden_act, w_two, preferred_element_type=jnp.float32).astype(jnp.bfloat16)

        z_tgt = jnp.einsum('td,td->t', query_vec, tgt_rows, preferred_element_type=jnp.float32)
        z_cand = jnp.einsum('td,sd->ts', query_vec, cand_rows, preferred_element_type=jnp.float32) - cand_logq[None, :]
        z_cand = jnp.where(y_blk[:, None] == cand_ids[None, :], -1e9, z_cand)
        peak_val = jnp.maximum(jnp.max(z_cand, axis=1), z_tgt)
        exp_total = jnp.exp(z_tgt - peak_val) + jnp.sum(jnp.exp(z_cand - peak_val[:, None]), axis=1)
        log_norm = peak_val + jnp.log(exp_total)
        loss_part = jnp.sum(log_norm - z_tgt)
        dz_tgt = (jnp.exp(z_tgt - log_norm) - 1.0) / total_tok
        dz_cand = (jnp.exp(z_cand - log_norm[:, None]) / total_tok).astype(jnp.bfloat16)
        d_query = (dz_tgt[:, None] * tgt_rows.astype(jnp.float32)
                   + jnp.dot(dz_cand, cand_rows, preferred_element_type=jnp.float32)).astype(jnp.bfloat16)

        note = jnp.concatenate([dz_tgt, jnp.broadcast_to(loss_part, (8 * lane - tok_dev,))]).reshape(8, lane)
        notes = spread(note, n, 4).reshape(n, 8 * lane)
        loss_val = jnp.sum(notes[:, tok_dev]) / total_tok
        query_all = lax.all_gather(query_vec.reshape(tok_dev, sub, lane), 'dp', tiled=True)

        part_cand = jnp.einsum('ts,td->sd', dz_cand, query_vec, preferred_element_type=jnp.float32)
        own_cand_grad = reduce_scatter(part_cand, n, 1)
        sent_cand, query_all = lax.optimization_barrier((own_cand_grad.reshape(cand_dev, sub, lane), query_all))
        cand_grad = lax.all_gather(sent_cand, 'dp', tiled=True)

        part_two = jnp.einsum('tf,td->fd', hidden_act, d_query, preferred_element_type=jnp.float32)
        part_two, own_cand_grad = lax.optimization_barrier((part_two, own_cand_grad))
        own_two = reduce_scatter(part_two, n, 2)
        sent_two, query_all = lax.optimization_barrier((own_two, query_all))
        grad_two = lax.all_gather(sent_two, 'dp', tiled=True)

        d_act = jnp.einsum('td,fd->tf', d_query, w_two, preferred_element_type=jnp.float32)
        d_pre = gelu_back(d_act.astype(jnp.bfloat16).astype(jnp.float32))[0].astype(jnp.bfloat16)
        part_one = outer(x_flip, d_pre)
        part_one, own_two = lax.optimization_barrier((part_one, own_two))
        own_one = reduce_scatter(part_one, n, 3)
        sent_one, cand_grad = lax.optimization_barrier((own_one, cand_grad))
        grad_one = lax.all_gather(sent_one, 'dp', tiled=True)

        grad_table = table_grad(keys, first, last, notes[:, :tok_dev].reshape(-1), query_all, cand_grad, rows_dev, n, count)
        return loss_val, grad_table, grad_one, grad_two

    return jax.shard_map(local_step, mesh=mesh,
                         in_specs=(P('dp', None), P(), P(), P('dp', None), P(), P(), P('dp')),
                         out_specs=(P(), P('dp', None), P(), P()), check_vma=False)
```

time: 1850 us -> 1070 us (0.58)
  waiting for transfers between devices: 1260 us -> 151 us
  Pallas kernels: 0 us -> 774 us
  other arithmetic: 229 us -> 6.24 us
  blocking collectives: 126 us -> 0 us
  local copies, waits for them, and re-layouts: 140 us -> 54.7 us
    psum x2 -> x0, waiting for transfers between devices: 821 us -> none  [the longest x1 639 us: local_step(): lax.psum(jnp.einsum('ts,td->sd', dz_cand, query_vec, preferred_element_ty...]
    pallas_call x0 -> x9, Pallas kernels: none -> 774 us  [the longest x4 639 us: reduce_scatter(): pl.pallas_call(functools.partial(reduce_kernel, tile, steps), out_shape=j...]
    reduce_scatter x1 -> x0, waiting for transfers between devices: 307 us -> none  [local_step(): tgt_rows = lax.psum_scatter(tgt_part, 'dp', scatter_dimension=0, tiled=True)]
    scatter-add x2 -> x0, other arithmetic: 196 us -> none  [the longest x1 152 us: local_step(): grad_table.at[tgt_slot]]
    gather x2, local copies, waits for them, and re-layouts: 110 us -> 3.61 us  [the longest x1 2.05 us: local_step(): tgt_rows = got.at[rank[:tok_dev]].get(mode='promise_in_bounds')]
    all_gather x2 -> x0, blocking collectives: 84.7 us -> none  [the longest x1 43.6 us: local_step(): all_targets = lax.all_gather(y_blk, 'dp', tiled=True)]
    psum x1 -> x0, blocking collectives: 41.6 us -> none  [local_step(): loss_val = lax.psum(jnp.sum(log_norm - z_tgt), 'dp') / total_tok]
    select_n x4 -> x2, other arithmetic: 31.5 us -> 1.21 us  [the longest x1 0.69 us: local_step(): tgt_rows = got.at[rank[:tok_dev]].get(mode='promise_in_bounds')]
  transfers between devices with their start and end apart: 4 -> 5, of which waited for: 4 -> 3; matrix products, arithmetic and copies ran while one was open for 6% -> 7% of each run, Pallas kernels for 0% -> 48%
where the time goes in v1:
time: 1070 us
  Pallas kernels  774 us (72%)
  waiting for transfers between devices  151 us (14%)
  matrix products  62 us (6%)
  local copies, waits for them, and re-layouts  54.7 us (5%)
  between operations  16.3 us (2%)
    pallas_call x4, Pallas kernels, reduce_scatter(): pl.pallas_call(functools.partial(reduce_kernel, tile, steps), out_shape=j...  639 us
    all_gather x1, waiting for transfers between devices, local_step(): lax.all_gather(query_vec.reshape(tok_dev, sub, lane), 'dp', tiled=True)  66.8 us
    pallas_call x1, Pallas kernels, table_grad(): pl.pallas_call(functools.partial(table_kernel, n, count, tok_dev, rows_de...  66.2 us
    all_gather x1, waiting for transfers between devices, local_step(): cand_rows = lax.all_gather(own_cand, 'dp', tiled=True)  56 us
    unnamed x57, local copies, waits for them, and re-layouts  48.4 us
    pallas_call x1, Pallas kernels, pick_rows(): pl.pallas_call(functools.partial(pick_kernel, n, count, table3.shape[0]),...  38.5 us
    all_gather x1, waiting for transfers between devices, local_step(): grad_one = lax.all_gather(sent_one, 'dp', tiled=True)  28.3 us
    pallas_call x2, Pallas kernels, spread(): pl.pallas_call(functools.partial(spread_kernel, n), out_shape=jax.ShapeDt...  21.7 us
  transfers between devices with their start and end apart: 5, of which 3 were waited for; matrix products, arithmetic and copies ran while one was open for 7% of the time, Pallas kernels for 48%

profile of v1, /device:TPU:0, one launch (start us, length us, event | category | flops | bytes accessed | tf_op | source)
XLA Modules:
  0.0 1066.0 jit_solution(7855379434454817372)
XLA Ops:
  10.7 12.0 %spread_0.1 = s32[32,8,128]{2,1,0:T(8,128)} custom-call(s32[8,128]{1,0:T(8,128)} %pad_bitcast_fusion.1.in_ref), custom_call_target="tpu_custom_call" | custom-call | tf_op jit(solution)/shard_map/spread_0/pallas_call | solution.py:42
  23.8 9.0 copy.20
  36.1 38.5 %pick_rows.1 = bf16[32,640,8,128]{3,2,1,0:T(8,128)(2,1)} custom-call(s32[20480]{0:T(1024)S(1)} %reshape.94.keys, s32[32]{0:T(128)S(1)} %get-tuple-element.21.first, s32[32]{0:T(128)S(1)} %get-tuple-element.20.last, bf16[4096,8,128]{2,1,0:T(8,128)(2,1)S(1)} %bitcast.41), custom_call_target="tpu_custom_call" | custom-call | tf_op jit(solution)/shard_map/pick_rows/pallas_call | solution.py:215
  74.7 210.8 %reduce_5.1 = bf16[640,8,128]{2,1,0:T(8,128)(2,1)} custom-call(bf16[16,2,640,8,128]{4,3,2,1,0:T(8,128)(2,1)} %bitcast.47), custom_call_target="tpu_custom_call" | custom-call | tf_op jit(solution)/shard_map/reduce_5/pallas_call | solution.py:153
  292.6 8.5 convolution_convert_fusion.1
  301.1 10.4 fusion.11
  314.4 56.0 %all-gather.15.cloned.1.call-done = bf16[4096,1024]{1,0:T(8,128)(2,1)} async-done(((bf16[128,1024]{1,0:T(8,128)(2,1)}), bf16[4096,1024]{1,0:T(8,128)(2,1)}) %all-gather.15.cloned.1.call-update) | async-done | bytes 8388624 | tf_op jit(solution)/shard_map/all_gather | solution.py:329
  370.4 7.6 fusion.19
  380.4 6.4 fusion.18
  386.9 144.4 %reduce_1.1 = f32[128,1024]{1,0:T(8,128)S(1)} custom-call(f32[16,2,128,1024]{3,2,1,0:T(8,128)S(1)} %bitcast.42), custom_call_target="tpu_custom_call" | custom-call | tf_op jit(solution)/shard_map/reduce_1/pallas_call | solution.py:153
  532.2 66.8 %all-gather.7.cloned.1.call-done.query = bf16[16384,8,128]{2,1,0:T(8,128)(2,1)} async-done(((bf16[512,8,128]{2,1,0:T(8,128)(2,1)}), bf16[16384,8,128]{2,1,0:T(8,128)(2,1)}) %all-gather.7.cloned.1.call-update) | async-done | bytes 33554448 | tf_op jit(solution)/shard_map/all_gather | solution.py:353
  599.2 10.5 fusion.13
  609.7 6.4 fusion.15
  616.2 144.0 %reduce_2.1 = f32[128,1024]{1,0:T(8,128)} custom-call(f32[16,2,128,1024]{3,2,1,0:T(8,128)S(1)} %bitcast.43), custom_call_target="tpu_custom_call" | custom-call | tf_op jit(solution)/shard_map/reduce_2/pallas_call | solution.py:153
  761.0 12.2 %fusion.3.right = bf16[512,4096]{1,0:T(8,128)(2,1)S(1)} fusion(bf16[512,4096]{1,0:T(8,128)(2,1)} %copy-done.19, bf16[512,1024]{1,0:T(8,128)(2,1)S(1)} %copy-done.22, bf16[4096,1024]{1,0:T(8,128)(2,1)} %param.9), kind=kOutput, calls=%fused_computation.11 | convolution fusion | flops 4343201792 | bytes 17825792 | tf_op jit(solution)/shard_map/td,fd->tf/dot_general | solution.py:366
  773.2 8.7 outer.1
  782.0 140.0 %reduce_3.1 = f32[32,4096]{1,0:T(8,128)} custom-call(f32[16,2,32,4096]{3,2,1,0:T(8,128)S(1)} %bitcast.40), custom_call_target="tpu_custom_call" | custom-call | tf_op jit(solution)/shard_map/reduce_3/pallas_call | solution.py:153
  923.2 9.7 spread_4.1
  935.3 5.8 copy-done.7
  941.0 66.2 %table_grad.1 = f32[4096,1024]{1,0:T(8,128)} custom-call(s32[20480]{0:T(1024)S(1)} %copy-done.2, s32[32]{0:T(128)S(1)} %copy-done.6, s32[32]{0:T(128)S(1)} %copy-done.4, f32[16384]{0:T(1024)S(1)} %bitcast.46, bf16[16384,8,128]{2,1,0:T(8,128)(2,1)} %all-gather.7.cloned.1.call-done.query, f32[4096,8,128]{2,1,0:T(8,128)S(1)} %copy-done.7), custom_call_target="tpu_custom_call" | custom-call | flops 30000001024 | bytes 67108864 | tf_op jit(solution)/shard_map/table_grad/pallas_call | solution.py:268
  1007.2 28.3 %all-gather.11.cloned.1.call-done = f32[1024,4096]{1,0:T(8,128)} async-done(((f32[32,4096]{1,0:T(8,128)}), f32[1024,4096]{1,0:T(8,128)}) %all-gather.11.cloned.1.call-update) | async-done | bytes 16777232 | tf_op jit(solution)/shard_map/all_gather | solution.py:372
  1035.5 12.6 %copy.34 = f32[1024,4096]{1,0:T(8,128)} copy(f32[1024,4096]{1,0:T(8,128)} %all-gather.11.cloned.1.call-done) | data formatting | bytes 33554432
  1048.1 3.8 copy-done.8
  1052.0 6.2 copy.35
  (83 shorter events, 25.1 us)
Async XLA Ops:
  7.2 363.2 %all-gather.15.cloned.1.call-start = ((), (), s32[]{:S(2)}) async-start(), calls=%async_computation.4 | async-start | bytes 8650752 | tf_op jit(solution)/shard_map/all_gather | solution.py:329
  23.7 9.0 copy-start.3
  23.7 9.0 copy-start.5
  23.7 9.0 copy-start.1
  285.4 7.1 copy-start.12
  289.5 309.5 %all-gather.7.cloned.1.call-start = ((), (), s32[]{:S(2)}) async-start(), calls=%async_computation | async-start | bytes 34603008 | tf_op jit(solution)/shard_map/all_gather | solution.py:353
  292.6 8.5 copy-start.10
  301.1 10.4 copy-start.19
  301.1 69.3 %copy-start.16 = (s32[512]{0:T(512)S(1)}, s32[512]{0:T(512)}, u32[]{:S(2)}) copy-start(s32[512]{0:T(512)} %param.13) | copy-start | bytes 6148
  301.1 69.3 %copy-start.17 = (s32[4096]{0:T(1024)S(1)}, s32[4096]{0:T(1024)}, u32[]{:S(2)}) copy-start(s32[4096]{0:T(1024)} %param.11) | copy-start | bytes 49156
  301.1 69.3 %copy-start.18 = (f32[4096]{0:T(1024)S(1)}, f32[4096]{0:T(1024)}, u32[]{:S(2)}) copy-start(f32[4096]{0:T(1024)} %param.12) | copy-start | bytes 49156
  313.8 608.2 %all-gather.9.cloned.1.call-start = ((), (), s32[]{:S(2)}) async-start(), calls=%async_computation.1 | async-start | bytes 17301504 | tf_op jit(solution)/shard_map/all_gather | solution.py:358
  378.0 8.8 copy-start.9
  386.9 212.4 %copy-start.11 = (bf16[512,1024]{1,0:T(8,128)(2,1)S(1)}, bf16[512,1024]{1,0:T(8,128)(2,1)}, u32[]{:S(2)}) copy-start(bf16[512,1024]{1,0:T(8,128)(2,1)} %copy-done.10) | copy-start | bytes 3145732
  599.0 336.2 %all-gather.13.cloned.1.call-start = ((), (), s32[]{:S(2)}) async-start(), calls=%async_computation.3 | async-start | bytes 17301504 | tf_op jit(solution)/shard_map/all_gather | solution.py:364
  599.2 10.5 copy-start.20
  609.7 6.4 copy-start.21
  616.2 144.3 %copy-start.13 = (bf16[512,1024]{1,0:T(8,128)(2,1)S(1)}, bf16[512,1024]{1,0:T(8,128)(2,1)}, u32[]{:S(2)}) copy-start(bf16[512,1024]{1,0:T(8,128)(2,1)} %param.7) | copy-start | bytes 3145732
  616.2 144.9 %copy-start.22 = (bf16[512,1024]{1,0:T(8,128)(2,1)S(1)}, bf16[512,1024]{1,0:T(8,128)(2,1)}, u32[]{:S(2)}) copy-start(bf16[512,1024]{1,0:T(8,128)(2,1)} %copy-done.21) | copy-start | bytes 3145732
  760.2 275.3 %all-gather.11.cloned.1.call-start = ((), (), s32[]{:S(2)}) async-start(), calls=%async_computation.2 | async-start | bytes 17301504 | tf_op jit(solution)/shard_map/all_gather | solution.py:372
  781.9 153.3 %copy-start.2 = (s32[20480]{0:T(1024)S(1)}, s32[20480]{0:T(1024)}, u32[]{:S(2)}) copy-start(s32[20480]{0:T(1024)} %copy-done.1) | copy-start | bytes 245764
  782.0 153.3 %copy-start.4 = (s32[32]{0:T(128)S(1)}, s32[32]{0:T(128)}, u32[]{:S(2)}) copy-start(s32[32]{0:T(128)} %copy-done.3) | copy-start | bytes 388
  782.0 153.3 %copy-start.6 = (s32[32]{0:T(128)S(1)}, s32[32]{0:T(128)}, u32[]{:S(2)}) copy-start(s32[32]{0:T(128)} %copy-done.5) | copy-start | bytes 388
  1035.5 16.4 %copy-start.8 = (f32[4096,1024]{1,0:T(8,128)S(1)}, f32[4096,1024]{1,0:T(8,128)}, u32[]{:S(2)}) copy-start(f32[4096,1024]{1,0:T(8,128)} %all-gather.13.cloned.1.call-done) | copy-start | bytes 50331652
  (4 other events, 10.7 us)
Sparse Core Ops, SparseCore 0:
  289.6 80.7 all-gather.14
  373.2 225.6 all-gather.6
  602.4 149.7 all-gather.8
  760.3 151.1 all-gather.12
  922.1 113.3 all-gather.10

commit v2 on v1

--- a/solution.py
+++ b/solution.py
@@ -56,15 +56,23 @@
     core = lax.rem(me, 2)
     xb, yb = lax.rem(me // 2, 2), lax.rem(me // 4, 2)
     z0, z1 = lax.rem(me // 8, 2), lax.rem(me // 16, 2)
-    w1, w2 = 1 + core, 2 - core
-    b1 = xb * (1 - core) + yb * core
-    b2 = yb * (1 - core) + xb * core
-    bits = (core, b1, b2, z0, z1)
-    mates = [me + 2 * w * (1 - 2 * b) for b, w in zip(bits[1:], (w1, w2, 4, 8))]
-    mates = ([me + 1 - 2 * core] + mates)[:steps]
+    one = (1 + core, xb * (1 - core) + yb * core)
+    two = (2 - core, yb * (1 - core) + xb * core)
+    ways = ((one, two, (4, z0), (8, z1))[:steps - 1], ((4, z0), (8, z1), one, two)[-steps + 1:] if steps > 4 else ((4, z0), one, two))
+
+    def way(part):
+        return ways[1 if part % 4 == 1 else 0]
+
+    def mate(step, part):
+        if step == 0:
+            return me + 1 - 2 * core
+        weight, bit = way(part)[step - 1]
+        return me + 2 * weight * (1 - 2 * bit)
+
+    mates = [mate(step, 0) for step in range(steps)]
     barrier = pltpu.get_barrier_semaphore()
-    for mate in mates:
-        pl.semaphore_signal(barrier, inc=1, device_id=(mate,), device_id_type=MESH)
+    for other in mates:
+        pl.semaphore_signal(barrier, inc=1, device_id=(other,), device_id_type=MESH)
 
     def piece(part):
         if tile[0] is None:
@@ -78,30 +86,29 @@
         load(part).start()
     pl.semaphore_wait(barrier, steps)
 
-    def place(step, i, bit):
-        if step == 1:
-            return bit * w1 + lax.rem(i, 2) * w2 + (i // 2) * 4
-        base = b1 * w1
-        if step == 2:
-            return base + bit * w2 + i * 4
-        base = base + b2 * w2
-        if step == 3:
-            return base + bit * 4 + i * 8
-        return base + z0 * 4 + bit * 8
+    def place(step, part, i, theirs):
+        dims = way(part)
+        weight, bit = dims[step - 1]
+        at = weight * (1 - bit if theirs else bit)
+        for w, own in dims[:step - 1]:
+            at = at + w * own
+        for k, (w, _) in enumerate(dims[step:]):
+            at = at + w * lax.rem(i // 2 ** k, 2)
+        return at
 
     def send(step, part):
         if step == 0:
             pltpu.make_async_remote_copy(
                 src_ref=in_ref.at[(slice(None), 1 - core) + piece(part)], dst_ref=got[0].at[part],
                 send_sem=send_sem.at[0, part], recv_sem=recv_sem.at[0, part],
-                device_id=(mates[0],), device_id_type=MESH).start()
+                device_id=(mate(0, part),), device_id_type=MESH).start()
             return
 
         def one(i, carry):
             pltpu.make_async_remote_copy(
-                src_ref=acc.at[part, place(step, i, 1 - bits[step])], dst_ref=got[step].at[part, i],
+                src_ref=acc.at[part, place(step, part, i, True)], dst_ref=got[step].at[part, i],
                 send_sem=send_sem.at[step, part], recv_sem=recv_sem.at[step, part],
-                device_id=(mates[step],), device_id_type=MESH).start()
+                device_id=(mate(step, part),), device_id_type=MESH).start()
             return carry
         lax.fori_loop(0, got[step].shape[1], one, 0)
 
@@ -109,11 +116,11 @@
         return pltpu.make_async_remote_copy(
             src_ref=got[step].at[part], dst_ref=got[step].at[part],
             send_sem=send_sem.at[step, part], recv_sem=recv_sem.at[step, part],
-            device_id=(mates[step],), device_id_type=MESH)
+            device_id=(mate(step, part),), device_id_type=MESH)
 
     def add(step, part):
         def one(i, carry):
-            at = i if step == 0 else place(step, i, bits[step])
+            at = i if step == 0 else place(step, part, i, False)
             acc[part, at] = acc[part, at] + got[step][part, i]
             return carry
         lax.fori_loop(0, got[step].shape[1], one, 0)
@@ -122,7 +129,9 @@
         return pltpu.make_async_copy(acc.at[part, me // 2], out_ref.at[piece(part)], store_sem.at[part])
 
     for tick in range(PARTS + steps):
-        for step in range(steps - 1, -1, -1):
+        if tick < PARTS:
+            send(0, tick)
+        for step in range(steps):
             part = tick - 1 - step
             if 0 <= part < PARTS:
                 if step == 0:
@@ -133,8 +142,6 @@
                     send(step + 1, part)
                 else:
                     store(part).start()
-        if tick < PARTS:
-            send(0, tick)
     for part in range(PARTS):
         for step in range(steps):
             whole(step, part).wait_send()
@@ -171,53 +178,61 @@
 OUT_ROWS = 256
 
 
-def pick_kernel(n, count, rows_dev, keys, first, last, table, rows_out, buf, sems):
+def pick_kernel(n, count, rows_dev, keys, first, last, table, tgt_out, cand_out, buf, sems):
     base = lax.axis_index('dp') * rows_dev
+    tok_dev = tgt_out.shape[1]
 
     def zero(i, carry):
-        for slot in range(2):
-            buf[slot, pl.ds(i * 32, 32)] = jnp.zeros((32,) + buf.shape[2:], buf.dtype)
+        for side in range(2):
+            buf[side, pl.ds(i * 32, 32)] = jnp.zeros((32,) + buf.shape[2:], buf.dtype)
         return carry
 
     lax.fori_loop(0, count // 32, zero, 0)
 
-    def out_copy(j, slot):
-        return pltpu.make_async_copy(buf.at[slot], rows_out.at[j], sems.at[slot])
+    def out_copies(j, side):
+        return (pltpu.make_async_copy(buf.at[side, pl.ds(0, tok_dev)], tgt_out.at[j], sems.at[side, 0]),
+                pltpu.make_async_copy(buf.at[side, pl.ds(tok_dev, count - tok_dev)], cand_out.at[j], sems.at[side, 1]))
 
     def per_dev(j, carry):
-        slot = lax.rem(j, 2)
+        side = lax.rem(j, 2)
 
         @pl.when(j >= 2)
         def _():
-            out_copy(j - 2, slot).wait()
+            for copy in out_copies(j - 2, side):
+                copy.wait()
 
             def clear(i, c):
-                buf[slot, i] = jnp.zeros(buf.shape[2:], buf.dtype)
+                buf[side, lax.rem(keys[(j - 2) * count + i], SLOT_BITS)] = jnp.zeros(buf.shape[2:], buf.dtype)
                 return c
 
             lax.fori_loop(first[j - 2], last[j - 2], clear, 0)
 
         def one(i, c):
-            buf[slot, i] = table[keys[j * count + i] // SLOT_BITS - base]
+            key = keys[j * count + i]
+            buf[side, lax.rem(key, SLOT_BITS)] = table[key // SLOT_BITS - base]
             return c
 
         lax.fori_loop(first[j], last[j], one, 0)
-        out_copy(j, slot).start()
+        for copy in out_copies(j, side):
+            copy.start()
         return carry
 
     lax.fori_loop(0, n, per_dev, 0)
-    out_copy(n - 2, 0).wait()
-    out_copy(n - 1, 1).wait()
-
-
-def pick_rows(table3, keys, first, last, n, count):
+    for copy in out_copies(n - 2, 0) + out_copies(n - 1, 1):
+        copy.wait()
+
+
+def pick_rows(table3, keys, first, last, n, count, tok_dev):
     smem = pl.BlockSpec(memory_space=pltpu.SMEM)
+    anywhere = pl.BlockSpec(memory_space=pl.ANY)
+    tail = table3.shape[1:]
     return pl.pallas_call(
         functools.partial(pick_kernel, n, count, table3.shape[0]),
-        out_shape=jax.ShapeDtypeStruct((n, count) + table3.shape[1:], table3.dtype),
+        out_shape=(jax.ShapeDtypeStruct((n, tok_dev) + tail, table3.dtype),
+                   jax.ShapeDtypeStruct((n, count - tok_dev) + tail, table3.dtype)),
         in_specs=[smem, smem, smem, pl.BlockSpec(memory_space=pltpu.VMEM)],
-        out_specs=pl.BlockSpec(memory_space=pl.ANY),
-        scratch_shapes=[pltpu.VMEM((2, count) + table3.shape[1:], table3.dtype), pltpu.SemaphoreType.DMA((2,))],
+        out_specs=(anywhere, anywhere),
+        scratch_shapes=[pltpu.VMEM((2, count) + tail, table3.dtype), pltpu.SemaphoreType.DMA((2, 2))],
         compiler_params=pltpu.CompilerParams(vmem_limit_bytes=24 * 2**20),
         name='pick_rows',
     )(keys, first, last, table3)
@@ -323,17 +338,18 @@
         last = jnp.sum((everyone - me * rows_dev * SLOT_BITS < rows_dev * SLOT_BITS).astype(jnp.int32), axis=1)
         keys = everyone.reshape(-1)
 
-        picked = pick_rows(table_blk.reshape(rows_dev, sub, lane), keys, first, last, n, count)
-        got = reduce_scatter(picked.reshape(n * count, sub, lane), n, 5).reshape(count, emb_dim)
-        own_cand = got.at[rank[tok_dev:]].get(mode='promise_in_bounds')
+        tgt_part, cand_part = pick_rows(table_blk.reshape(rows_dev, sub, lane), keys, first, last, n, count, tok_dev)
+        own_cand = reduce_scatter(cand_part.reshape(n * cand_dev, sub, lane), n, 5).reshape(cand_dev, emb_dim)
         cand_rows = lax.all_gather(own_cand, 'dp', tiled=True)
-        tgt_rows = got.at[rank[:tok_dev]].get(mode='promise_in_bounds')
 
         x_flip = lax.optimization_barrier(x_blk.T)
         pre_act = jnp.dot(x_blk, w_one, preferred_element_type=jnp.float32).astype(jnp.bfloat16)
         act_val, gelu_back = jax.vjp(jax.nn.gelu, pre_act.astype(jnp.float32))
         hidden_act = act_val.astype(jnp.bfloat16)
         query_vec = jnp.dot(hidden_act, w_two, preferred_element_type=jnp.float32).astype(jnp.bfloat16)
+        query_all = lax.all_gather(query_vec.reshape(tok_dev, sub, lane), 'dp', tiled=True)
+        tgt_part, query_vec = lax.optimization_barrier((tgt_part, query_vec))
+        tgt_rows = reduce_scatter(tgt_part.reshape(n * tok_dev, sub, lane), n, 6).reshape(tok_dev, emb_dim)
 
         z_tgt = jnp.einsum('td,td->t', query_vec, tgt_rows, preferred_element_type=jnp.float32)
         z_cand = jnp.einsum('td,sd->ts', query_vec, cand_rows, preferred_element_type=jnp.float32) - cand_logq[None, :]
@@ -350,8 +366,6 @@
         note = jnp.concatenate([dz_tgt, jnp.broadcast_to(loss_part, (8 * lane - tok_dev,))]).reshape(8, lane)
         notes = spread(note, n, 4).reshape(n, 8 * lane)
         loss_val = jnp.sum(notes[:, tok_dev]) / total_tok
-        query_all = lax.all_gather(query_vec.reshape(tok_dev, sub, lane), 'dp', tiled=True)
-
         part_cand = jnp.einsum('ts,td->sd', dz_cand, query_vec, preferred_element_type=jnp.float32)
         own_cand_grad = reduce_scatter(part_cand, n, 1)
         sent_cand, query_all = lax.optimization_barrier((own_cand_grad.reshape(cand_dev, sub, lane), query_all))

time: 1070 us -> 1040 us (0.972)
  waiting for transfers between devices: 151 us -> 38.2 us
  Pallas kernels: 774 us -> 855 us
    pallas_call x4 -> x5, Pallas kernels: 639 us -> 711 us  [reduce_scatter(): pl.pallas_call(functools.partial(reduce_kernel, tile, steps), out_shape=j...]
    all_gather x1, waiting for transfers between devices: 66.8 us -> 0.01 us  [local_step(): lax.all_gather(query_vec.reshape(tok_dev, sub, lane), 'dp', tiled=True)]
    all_gather x1, waiting for transfers between devices: 56 us -> 0.01 us  [local_step(): cand_rows = lax.all_gather(own_cand, 'dp', tiled=True)]
    unnamed x57 -> x31, local copies, waits for them, and re-layouts: 48.4 us -> 47.1 us
  transfers between devices with their start and end apart: 5 -> 5, of which waited for: 3 -> 1; matrix products, arithmetic and copies ran while one was open for 7% -> 7% of each run, Pallas kernels for 48% -> 73%
where the time goes in v2:
time: 1040 us; the launch traced here: 1030 us
  Pallas kernels  855 us (82%)
  matrix products  62.1 us (6%)
  local copies, waits for them, and re-layouts  49.7 us (5%)
  waiting for transfers between devices  38.2 us (4%)
  between operations  16.3 us (2%)
    pallas_call x5, Pallas kernels, reduce_scatter(): pl.pallas_call(functools.partial(reduce_kernel, tile, steps), out_shape=j...  711 us
    pallas_call x1, Pallas kernels, table_grad(): pl.pallas_call(functools.partial(table_kernel, n, count, tok_dev, rows_de...  65.2 us
    unnamed x31, local copies, waits for them, and re-layouts  47.1 us
    pallas_call x1, Pallas kernels, pick_rows(): pl.pallas_call(functools.partial(pick_kernel, n, count, table3.shape[0]),...  44.1 us
    all_gather x1, waiting for transfers between devices, local_step(): grad_one = lax.all_gather(sent_one, 'dp', tiled=True)  38.1 us
    pallas_call x2, Pallas kernels, spread(): pl.pallas_call(functools.partial(spread_kernel, n), out_shape=jax.ShapeDt...  26 us
  transfers between devices with their start and end apart: 5, of which 1 were waited for; matrix products, arithmetic and copies ran while one was open for 7% of the time, Pallas kernels for 73%

profile of v2, /device:TPU:0, one launch (start us, length us, event | category | flops | bytes accessed | tf_op | source)
XLA Modules:
  0.0 1026.5 jit_solution(8964765453957398673)
XLA Ops:
  9.8 11.9 %spread_0.1 = s32[32,8,128]{2,1,0:T(8,128)} custom-call(s32[8,128]{1,0:T(8,128)} %pad_bitcast_fusion.1.in_ref), custom_call_target="tpu_custom_call" | custom-call | tf_op jit(solution)/shard_map/spread_0/pallas_call | solution.py:42
  22.9 8.9 copy.20
  31.8 3.4 copy-done
  35.2 44.1 %pick_rows.1 = (bf16[32,512,8,128]{3,2,1,0:T(8,128)(2,1)}, bf16[32,128,8,128]{3,2,1,0:T(8,128)(2,1)S(1)}) custom-call(s32[20480]{0:T(1024)S(1)} %reshape.97.keys, s32[32]{0:T(128)S(1)} %get-tuple-element.29.first, s32[32]{0:T(128)S(1)} %get-tuple-element.28.last, bf16[4096,8,128]{2,1,0:T(8,128)(2,1)S(1)} %bitcast.46), custom_call_target="tpu_custom_call" | custom-call | tf_op jit(solution)/shard_map/pick_rows/pallas_call | solution.py:229
  79.3 52.2 %reduce_5.1 = bf16[128,8,128]{2,1,0:T(8,128)(2,1)S(1)} custom-call(bf16[16,2,128,8,128]{4,3,2,1,0:T(8,128)(2,1)S(1)} %bitcast.49), custom_call_target="tpu_custom_call" | custom-call | tf_op jit(solution)/shard_map/reduce_5/pallas_call | solution.py:160
  132.3 8.2 convolution_convert_fusion.1
  140.5 10.2 convolution_convert_fusion.2
  152.3 235.7 %reduce_6.1 = bf16[512,8,128]{2,1,0:T(8,128)(2,1)S(1)} custom-call(bf16[16,2,512,8,128]{4,3,2,1,0:T(8,128)(2,1)} %bitcast.56), custom_call_target="tpu_custom_call" | custom-call | tf_op jit(solution)/shard_map/reduce_6/pallas_call | solution.py:160
  388.4 7.3 fusion.19
  399.2 7.3 fusion.18
  406.5 158.1 %reduce_1.1 = f32[128,1024]{1,0:T(8,128)S(1)} custom-call(f32[16,2,128,1024]{3,2,1,0:T(8,128)S(1)} %bitcast.47), custom_call_target="tpu_custom_call" | custom-call | tf_op jit(solution)/shard_map/reduce_1/pallas_call | solution.py:160
  565.8 10.5 %fusion.13 = bf16[512,1024]{1,0:T(8,128)(2,1)S(1)} fusion(bf16[4096,1024]{1,0:T(8,128)(2,1)} %all-gather.6.cloned.1.call-done, f32[512]{0:T(512)S(1)} %add_multiply_fusion.1, bf16[64,8,8,128]{3,2,1,0:T(8,128)(2,1)S(1)} %bitcast.51, f32[512,4096]{1,0:T(8,128)} %copy-done.3, f32[512]{0:T(512)S(1)} %get-tuple-element.31), kind=kOutput, calls=%fused_computation.26 | convolution fusion | flops 4303355904 | bytes 18878464 | tf_op jit(solution)/shard_map/dot_general | solution.py:364
  576.3 6.4 fusion.15
  582.6 135.1 %reduce_2.1 = f32[128,1024]{1,0:T(8,128)} custom-call(f32[16,2,128,1024]{3,2,1,0:T(8,128)S(1)} %bitcast.48), custom_call_target="tpu_custom_call" | custom-call | tf_op jit(solution)/shard_map/reduce_2/pallas_call | solution.py:160
  718.6 12.2 %fusion.3.right = bf16[512,4096]{1,0:T(8,128)(2,1)S(1)} fusion(bf16[512,4096]{1,0:T(8,128)(2,1)} %copy-done.8, bf16[512,1024]{1,0:T(8,128)(2,1)S(1)} %fusion.13, bf16[4096,1024]{1,0:T(8,128)(2,1)} %param.9), kind=kOutput, calls=%fused_computation.9 | convolution fusion | flops 4343201792 | bytes 17825792 | tf_op jit(solution)/shard_map/td,fd->tf/dot_general | solution.py:380
  730.8 8.7 outer.1
  739.5 129.7 %reduce_3.1 = f32[32,4096]{1,0:T(8,128)} custom-call(f32[16,2,32,4096]{3,2,1,0:T(8,128)S(1)} %bitcast.45), custom_call_target="tpu_custom_call" | custom-call | tf_op jit(solution)/shard_map/reduce_3/pallas_call | solution.py:160
  870.5 14.1 %spread_4.1 = f32[32,8,128]{2,1,0:T(8,128)} custom-call(f32[8,128]{1,0:T(8,128)} %pad_bitcast_fusion.in_ref), custom_call_target="tpu_custom_call" | custom-call | tf_op jit(solution)/shard_map/spread_4/pallas_call | solution.py:42
  886.8 5.8 copy-done.1
  892.6 65.2 %table_grad.1 = f32[4096,1024]{1,0:T(8,128)} custom-call(s32[20480]{0:T(1024)S(1)} %reshape.97.keys, s32[32]{0:T(128)S(1)} %get-tuple-element.29.first, s32[32]{0:T(128)S(1)} %get-tuple-element.28.last, f32[16384]{0:T(1024)S(1)} %bitcast.55, bf16[16384,8,128]{2,1,0:T(8,128)(2,1)} %all-gather.8.cloned.1.call-done.query, f32[4096,8,128]{2,1,0:T(8,128)S(1)} %copy-done.1), custom_call_target="tpu_custom_call" | custom-call | flops 30000001024 | bytes 67108864 | tf_op jit(solution)/shard_map/table_grad/pallas_call | solution.py:283
  957.8 38.1 %all-gather.12.cloned.1.call-done = f32[1024,4096]{1,0:T(8,128)} async-done(((f32[32,4096]{1,0:T(8,128)}), f32[1024,4096]{1,0:T(8,128)}) %all-gather.12.cloned.1.call-update) | async-done | bytes 16777232 | tf_op jit(solution)/shard_map/all_gather | solution.py:386
  995.9 12.6 %copy.37 = f32[1024,4096]{1,0:T(8,128)} copy(f32[1024,4096]{1,0:T(8,128)} %all-gather.12.cloned.1.call-done) | data formatting | bytes 33554432
  1008.5 3.8 copy-done.2
  1012.3 6.2 copy.38
  (53 shorter events, 14.7 us)
Async XLA Ops:
  7.2 381.2 %all-gather.6.cloned.1.call-start = ((), (), s32[]{:S(2)}) async-start(), calls=%async_computation | async-start | bytes 8650752 | tf_op jit(solution)/shard_map/all_gather | solution.py:343
  31.8 3.4 copy-start
  35.2 97.1 %copy-start.4 = (bf16[512,1024]{1,0:T(8,128)(2,1)S(1)}, bf16[512,1024]{1,0:T(8,128)(2,1)}, u32[]{:S(2)}) copy-start(bf16[512,1024]{1,0:T(8,128)(2,1)} %param.7) | copy-start | bytes 3145732
  132.3 433.2 %all-gather.8.cloned.1.call-start = ((), (), s32[]{:S(2)}) async-start(), calls=%async_computation.1 | async-start | bytes 34603008 | tf_op jit(solution)/shard_map/all_gather | solution.py:350
  140.5 10.3 %copy-start.8 = (bf16[512,4096]{1,0:T(8,128)(2,1)}, bf16[512,4096]{1,0:T(8,128)(2,1)S(1)}, u32[]{:S(2)}) copy-start(bf16[512,4096]{1,0:T(8,128)(2,1)S(1)} %convolution_convert_fusion.1) | copy-start | bytes 12582916
  152.1 717.1 %all-gather.10.cloned.1.call-start = ((), (), s32[]{:S(2)}) async-start(), calls=%async_computation.2 | async-start | bytes 17301504 | tf_op jit(solution)/shard_map/all_gather | solution.py:372
  152.3 236.1 %copy-start.5 = (s32[512]{0:T(512)S(1)}, s32[512]{0:T(512)}, u32[]{:S(2)}) copy-start(s32[512]{0:T(512)} %param.13) | copy-start | bytes 6148
  152.3 236.1 %copy-start.6 = (s32[4096]{0:T(1024)S(1)}, s32[4096]{0:T(1024)}, u32[]{:S(2)}) copy-start(s32[4096]{0:T(1024)} %param.11) | copy-start | bytes 49156
  152.3 236.1 %copy-start.7 = (f32[4096]{0:T(1024)S(1)}, f32[4096]{0:T(1024)}, u32[]{:S(2)}) copy-start(f32[4096]{0:T(1024)} %param.12) | copy-start | bytes 49156
  395.8 3.4 copy-start.3
  565.5 321.3 %all-gather.14.cloned.1.call-start = ((), (), s32[]{:S(2)}) async-start(), calls=%async_computation.4 | async-start | bytes 17301504 | tf_op jit(solution)/shard_map/all_gather | solution.py:378
  565.8 10.5 %copy-start.9 = (bf16[512,4096]{1,0:T(8,128)(2,1)S(1)}, bf16[512,4096]{1,0:T(8,128)(2,1)}, u32[]{:S(2)}) copy-start(bf16[512,4096]{1,0:T(8,128)(2,1)} %copy-done.8) | copy-start | bytes 12582916
  717.7 278.1 %all-gather.12.cloned.1.call-start = ((), (), s32[]{:S(2)}) async-start(), calls=%async_computation.3 | async-start | bytes 17301504 | tf_op jit(solution)/shard_map/all_gather | solution.py:386
  886.8 5.8 copy-start.1
  995.8 16.4 %copy-start.2 = (f32[4096,1024]{1,0:T(8,128)S(1)}, f32[4096,1024]{1,0:T(8,128)}, u32[]{:S(2)}) copy-start(f32[4096,1024]{1,0:T(8,128)} %all-gather.14.cloned.1.call-done) | copy-start | bytes 50331652
Sparse Core Ops, SparseCore 0:
  132.4 105.1 all-gather.5
  241.1 297.9 all-gather.7
  565.6 153.6 all-gather.9
  722.1 157.4 all-gather.13
  882.3 113.4 all-gather.11

commit v3 on v2

--- a/solution.py
+++ b/solution.py
@@ -8,7 +8,7 @@
 from jax.sharding import PartitionSpec as P
 
 MESH = pl.DeviceIdType.MESH
-PARTS = 8
+PARTS = 16
 
 
 def spread_kernel(n, in_ref, out_ref, send_sem, recv_sem):
@@ -58,10 +58,14 @@
     z0, z1 = lax.rem(me // 8, 2), lax.rem(me // 16, 2)
     one = (1 + core, xb * (1 - core) + yb * core)
     two = (2 - core, yb * (1 - core) + xb * core)
-    ways = ((one, two, (4, z0), (8, z1))[:steps - 1], ((4, z0), (8, z1), one, two)[-steps + 1:] if steps > 4 else ((4, z0), one, two))
+    plain = (one, two, (4, z0), (8, z1))[:steps - 1]
+    turned = ((4, z0), (8, z1), one, two) if steps > 4 else ((4, z0), one, two)
 
     def way(part):
-        return ways[1 if part % 4 == 1 else 0]
+        flip = 1 if isinstance(part, int) and part % 4 == 1 else 0
+        if not isinstance(part, int):
+            flip = (lax.rem(part, 4) + 3) // 4 * (1 - lax.rem(part, 4) // 2)
+        return [(p + flip * (t - p), q + flip * (u - q)) for (p, q), (t, u) in zip(plain, turned)]
 
     def mate(step, part):
         if step == 0:
@@ -76,14 +80,17 @@
 
     def piece(part):
         if tile[0] is None:
-            return (slice(None), pl.ds(part * tile[1], tile[1]))
-        return (pl.ds(part * tile[0], tile[0]),)
+            return (slice(None), pl.ds(pl.multiple_of(part * tile[1], tile[1]), tile[1]))
+        return (pl.ds(pl.multiple_of(part * tile[0], tile[0]), tile[0]),)
 
     def load(part):
         return pltpu.make_async_copy(in_ref.at[(slice(None), core) + piece(part)], acc.at[part], load_sem.at[part])
 
-    for part in range(PARTS):
+    def begin(part, carry):
         load(part).start()
+        return carry
+
+    lax.fori_loop(0, PARTS, begin, 0)
     pl.semaphore_wait(barrier, steps)
 
     def place(step, part, i, theirs):
@@ -128,12 +135,16 @@
     def store(part):
         return pltpu.make_async_copy(acc.at[part, me // 2], out_ref.at[piece(part)], store_sem.at[part])
 
-    for tick in range(PARTS + steps):
-        if tick < PARTS:
-            send(0, tick)
+    def tick(t, carry):
+        @pl.when(t < PARTS)
+        def _():
+            send(0, t)
+
         for step in range(steps):
-            part = tick - 1 - step
-            if 0 <= part < PARTS:
+            part = t - 1 - step
+
+            @pl.when((part >= 0) & (part < PARTS))
+            def _():
                 if step == 0:
                     load(part).wait()
                 whole(step, part).wait_recv()
@@ -142,10 +153,18 @@
                     send(step + 1, part)
                 else:
                     store(part).start()
-    for part in range(PARTS):
+
+        return carry
+
+    lax.fori_loop(0, PARTS + steps, tick, 0)
+
+    def finish(part, carry):
         for step in range(steps):
             whole(step, part).wait_send()
         store(part).wait()
+        return carry
+
+    lax.fori_loop(0, PARTS, finish, 0)
 
 
 def reduce_scatter(x, n, cid):
@@ -302,7 +321,7 @@
 def outer(left, right):
     rows, depth = left.shape
     cols = right.shape[1]
-    high, wide = rows // 2, cols // 8
+    high, wide = rows, cols // 8
     return pl.pallas_call(
         outer_kernel,
         grid=(rows // high, cols // wide),
@@ -313,6 +332,42 @@
         compiler_params=pltpu.CompilerParams(vmem_limit_bytes=16 * 2**20),
         name='outer',
     )(left, right)
+
+
+def carry_kernel(in_ref, out_ref):
+    out_ref[...] = in_ref[...]
+
+
+def carry_over(x):
+    rows, cols = x.shape
+    spec = pl.BlockSpec((rows // 8, cols), lambda i: (i, 0))
+    return pl.pallas_call(
+        carry_kernel, grid=(8,), out_shape=jax.ShapeDtypeStruct(x.shape, x.dtype), in_specs=[spec], out_specs=spec,
+        cost_estimate=pl.CostEstimate(flops=x.size, bytes_accessed=8 * x.size, transcendentals=0),
+        compiler_params=pltpu.CompilerParams(vmem_limit_bytes=16 * 2**20), name='carry_over')(x)
+
+
+def fill_low(x):
+    rows, cols = x.shape
+    spec = pl.BlockSpec((rows // 4, cols), lambda i: (i, 0))
+    return pl.pallas_call(
+        carry_kernel, grid=(4,), out_shape=jax.ShapeDtypeStruct((2 * rows, cols), x.dtype), in_specs=[spec], out_specs=spec,
+        cost_estimate=pl.CostEstimate(flops=x.size, bytes_accessed=8 * x.size, transcendentals=0),
+        compiler_params=pltpu.CompilerParams(vmem_limit_bytes=16 * 2**20), name='fill_low')(x)
+
+
+def high_kernel(whole_ref, in_ref, out_ref):
+    out_ref[...] = in_ref[...]
+
+
+def fill_high(whole, x):
+    rows, cols = x.shape
+    return pl.pallas_call(
+        high_kernel, grid=(4,), out_shape=jax.ShapeDtypeStruct(whole.shape, x.dtype),
+        in_specs=[pl.BlockSpec(memory_space=pl.ANY), pl.BlockSpec((rows // 4, cols), lambda i: (i, 0))],
+        out_specs=pl.BlockSpec((rows // 4, cols), lambda i: (i + 4, 0)), input_output_aliases={0: 0},
+        cost_estimate=pl.CostEstimate(flops=x.size, bytes_accessed=8 * x.size, transcendentals=0),
+        compiler_params=pltpu.CompilerParams(vmem_limit_bytes=16 * 2**20), name='fill_high')(whole, x)
 
 
 def solution(mesh):
@@ -374,16 +429,24 @@
         part_two = jnp.einsum('tf,td->fd', hidden_act, d_query, preferred_element_type=jnp.float32)
         part_two, own_cand_grad = lax.optimization_barrier((part_two, own_cand_grad))
         own_two = reduce_scatter(part_two, n, 2)
-        sent_two, query_all = lax.optimization_barrier((own_two, query_all))
+        sent_two, cand_grad = lax.optimization_barrier((own_two, cand_grad))
         grad_two = lax.all_gather(sent_two, 'dp', tiled=True)
 
         d_act = jnp.einsum('td,fd->tf', d_query, w_two, preferred_element_type=jnp.float32)
         d_pre = gelu_back(d_act.astype(jnp.bfloat16).astype(jnp.float32))[0].astype(jnp.bfloat16)
-        part_one = outer(x_flip, d_pre)
-        part_one, own_two = lax.optimization_barrier((part_one, own_two))
-        own_one = reduce_scatter(part_one, n, 3)
-        sent_one, cand_grad = lax.optimization_barrier((own_one, cand_grad))
-        grad_one = lax.all_gather(sent_one, 'dp', tiled=True)
+        half = x_flip.shape[0] // 2
+        low = outer(x_flip[:half], d_pre)
+        low, own_two = lax.optimization_barrier((low, own_two))
+        own_low = reduce_scatter(low, n, 3)
+        sent_low, grad_two = lax.optimization_barrier((own_low, grad_two))
+        all_low = lax.all_gather(sent_low, 'dp', tiled=True)
+        high = outer(x_flip[half:], d_pre)
+        high, own_low = lax.optimization_barrier((high, own_low))
+        own_high = reduce_scatter(high, n, 7)
+        sent_high, all_low = lax.optimization_barrier((own_high, all_low))
+        all_high = lax.all_gather(sent_high, 'dp', tiled=True)
+        grad_one = fill_high(fill_low(all_low), all_high)
+        grad_two = carry_over(grad_two)
 
         grad_table = table_grad(keys, first, last, notes[:, :tok_dev].reshape(-1), query_all, cand_grad, rows_dev, n, count)
         return loss_val, grad_table, grad_one, grad_two

time: 1040 us -> 1100 us (1.058)
  Pallas kernels: 855 us -> 950 us
  waiting for transfers between devices: 38.2 us -> 15.5 us
    pallas_call x5 -> x6, Pallas kernels: 711 us -> 797 us  [reduce_scatter(): pl.pallas_call(functools.partial(reduce_kernel, tile, steps), out_shape=j...]
    all_gather x1 -> x2, waiting for transfers between devices: 38.1 us -> 0.02 us  [the longest x1 0.02 us: local_step(): all_low = lax.all_gather(sent_low, 'dp', tiled=True)]
    all_gather x1, waiting for transfers between devices: 0.02 us -> 15.4 us  [local_step(): grad_two = lax.all_gather(sent_two, 'dp', tiled=True)]
    pallas_call x0 -> x3, Pallas kernels: none -> 15.3 us  [the longest x1 8.05 us: carry_over(): pl.pallas_call(carry_kernel, grid=(8,), out_shape=jax.ShapeDtypeStruct(x....]
    unnamed x31 -> x37, local copies, waits for them, and re-layouts: 47.1 us -> 38.5 us
  transfers between devices with their start and end apart: 5 -> 6, of which waited for: 1 -> 1; matrix products, arithmetic and copies ran while one was open for 7% -> 6% of each run, Pallas kernels for 73% -> 75%
where the time goes in v3:
time: 1100 us; the launch traced here: 1090 us
  Pallas kernels  950 us (86%)
  matrix products  62 us (6%)
  local copies, waits for them, and re-layouts  41.1 us (4%)
  between operations  16.7 us (2%)
  waiting for transfers between devices  15.5 us (1%)
    pallas_call x6, Pallas kernels, reduce_scatter(): pl.pallas_call(functools.partial(reduce_kernel, tile, steps), out_shape=j...  797 us
    pallas_call x1, Pallas kernels, table_grad(): pl.pallas_call(functools.partial(table_kernel, n, count, tok_dev, rows_de...  64 us
    pallas_call x1, Pallas kernels, pick_rows(): pl.pallas_call(functools.partial(pick_kernel, n, count, table3.shape[0]),...  43.5 us
    unnamed x37, local copies, waits for them, and re-layouts  38.5 us
    pallas_call x2, Pallas kernels, spread(): pl.pallas_call(functools.partial(spread_kernel, n), out_shape=jax.ShapeDt...  22.1 us
  transfers between devices with their start and end apart: 6, of which 1 were waited for; matrix products, arithmetic and copies ran while one was open for 6% of the time, Pallas kernels for 75%

profile of v3, /device:TPU:0, one launch (start us, length us, event | category | flops | bytes accessed | tf_op | source)
XLA Modules:
  0.0 1091.4 jit_solution(12222812760061118186)
XLA Ops:
  9.8 11.9 %spread_0.1 = s32[32,8,128]{2,1,0:T(8,128)} custom-call(s32[8,128]{1,0:T(8,128)} %pad_bitcast_fusion.1.in_ref), custom_call_target="tpu_custom_call" | custom-call | tf_op jit(solution)/shard_map/spread_0/pallas_call | solution.py:42
  22.9 8.9 copy.21
  35.2 43.5 %pick_rows.1 = (bf16[32,512,8,128]{3,2,1,0:T(8,128)(2,1)}, bf16[32,128,8,128]{3,2,1,0:T(8,128)(2,1)S(1)}) custom-call(s32[20480]{0:T(1024)S(1)} %reshape.100.keys, s32[32]{0:T(128)S(1)} %get-tuple-element.35.first, s32[32]{0:T(128)S(1)} %get-tuple-element.34.last, bf16[4096,8,128]{2,1,0:T(8,128)(2,1)S(1)} %bitcast.46), custom_call_target="tpu_custom_call" | custom-call | tf_op jit(solution)/shard_map/pick_rows/pallas_call | solution.py:248
  78.7 67.5 %reduce_5.1 = bf16[128,8,128]{2,1,0:T(8,128)(2,1)S(1)} custom-call(bf16[16,2,128,8,128]{4,3,2,1,0:T(8,128)(2,1)S(1)} %bitcast.51), custom_call_target="tpu_custom_call" | custom-call | tf_op jit(solution)/shard_map/reduce_5/pallas_call | solution.py:179
  147.0 8.2 convolution_convert_fusion.1
  155.2 10.3 convolution_convert_fusion.2
  167.0 259.9 %reduce_6.1 = bf16[512,8,128]{2,1,0:T(8,128)(2,1)S(1)} custom-call(bf16[16,2,512,8,128]{4,3,2,1,0:T(8,128)(2,1)} %bitcast.57), custom_call_target="tpu_custom_call" | custom-call | tf_op jit(solution)/shard_map/reduce_6/pallas_call | solution.py:179
  427.4 7.3 fusion.20
  438.1 7.3 fusion.18
  445.4 136.2 %reduce_1.1 = f32[128,1024]{1,0:T(8,128)S(1)} custom-call(f32[16,2,128,1024]{3,2,1,0:T(8,128)S(1)} %bitcast.49), custom_call_target="tpu_custom_call" | custom-call | tf_op jit(solution)/shard_map/reduce_1/pallas_call | solution.py:179
  582.9 10.5 fusion.13
  593.3 6.4 fusion.15
  599.7 141.2 %reduce_2.1 = f32[128,1024]{1,0:T(8,128)} custom-call(f32[16,2,128,1024]{3,2,1,0:T(8,128)S(1)} %bitcast.50), custom_call_target="tpu_custom_call" | custom-call | tf_op jit(solution)/shard_map/reduce_2/pallas_call | solution.py:179
  741.9 12.1 %fusion.3.right = bf16[512,4096]{1,0:T(8,128)(2,1)S(1)} fusion(bf16[512,4096]{1,0:T(8,128)(2,1)} %copy-done.12, bf16[512,1024]{1,0:T(8,128)(2,1)S(1)} %fusion.13, bf16[4096,1024]{1,0:T(8,128)(2,1)} %param.9), kind=kOutput, calls=%fused_computation.9 | convolution fusion | flops 4343201792 | bytes 17825792 | tf_op jit(solution)/shard_map/td,fd->tf/dot_general | solution.py:435
  754.1 4.4 outer.3
  760.4 103.3 %reduce_3.1 = f32[16,4096]{1,0:T(8,128)} custom-call(f32[16,2,16,4096]{3,2,1,0:T(8,128)S(1)} %bitcast.48), custom_call_target="tpu_custom_call" | custom-call | tf_op jit(solution)/shard_map/reduce_3/pallas_call | solution.py:179
  863.7 15.4 %all-gather.13.cloned.1.call-done.in_ref = f32[4096,1024]{1,0:T(8,128)} async-done(((f32[128,1024]{1,0:T(8,128)}), f32[4096,1024]{1,0:T(8,128)}) %all-gather.13.cloned.1.call-update) | async-done | bytes 16777232 | tf_op jit(solution)/shard_map/all_gather | solution.py:433
  881.4 4.3 outer.2
  885.7 88.7 %reduce_7.1 = f32[16,4096]{1,0:T(8,128)} custom-call(f32[16,2,16,4096]{3,2,1,0:T(8,128)S(1)} %bitcast.47), custom_call_target="tpu_custom_call" | custom-call | tf_op jit(solution)/shard_map/reduce_7/pallas_call | solution.py:179
  975.8 10.1 spread_4.1
  988.1 5.8 copy-done.6
  993.9 64.0 %table_grad.1 = f32[4096,1024]{1,0:T(8,128)} custom-call(s32[20480]{0:T(1024)S(1)} %reshape.100.keys, s32[32]{0:T(128)S(1)} %get-tuple-element.35.first, s32[32]{0:T(128)S(1)} %get-tuple-element.34.last, f32[16384]{0:T(1024)S(1)} %bitcast.56, bf16[16384,8,128]{2,1,0:T(8,128)(2,1)} %all-gather.9.cloned.1.call-done.query, f32[4096,8,128]{2,1,0:T(8,128)S(1)} %copy-done.6), custom_call_target="tpu_custom_call" | custom-call | flops 30000001024 | bytes 67108864 | tf_op jit(solution)/shard_map/table_grad/pallas_call | solution.py:302
  1057.9 5.8 copy-done.3
  1063.7 8.0 carry_over.1
  (68 shorter events, 33.6 us)
Async XLA Ops:
  7.2 420.2 %all-gather.7.cloned.1.call-start = ((), (), s32[]{:S(2)}) async-start(), calls=%async_computation | async-start | bytes 8650752 | tf_op jit(solution)/shard_map/all_gather | solution.py:398
  31.8 3.4 copy-start
  35.2 111.8 %copy-start.8 = (bf16[512,1024]{1,0:T(8,128)(2,1)S(1)}, bf16[512,1024]{1,0:T(8,128)(2,1)}, u32[]{:S(2)}) copy-start(bf16[512,1024]{1,0:T(8,128)(2,1)} %param.7) | copy-start | bytes 3145732
  147.0 435.6 %all-gather.9.cloned.1.call-start = ((), (), s32[]{:S(2)}) async-start(), calls=%async_computation.1 | async-start | bytes 34603008 | tf_op jit(solution)/shard_map/all_gather | solution.py:405
  155.2 10.3 copy-start.12
  166.8 574.2 %all-gather.11.cloned.1.call-start = ((), (), s32[]{:S(2)}) async-start(), calls=%async_computation.2 | async-start | bytes 17301504 | tf_op jit(solution)/shard_map/all_gather | solution.py:427
  167.0 260.3 %copy-start.9 = (s32[512]{0:T(512)S(1)}, s32[512]{0:T(512)}, u32[]{:S(2)}) copy-start(s32[512]{0:T(512)} %param.13) | copy-start | bytes 6148
  167.0 260.3 %copy-start.10 = (s32[4096]{0:T(1024)S(1)}, s32[4096]{0:T(1024)}, u32[]{:S(2)}) copy-start(s32[4096]{0:T(1024)} %param.11) | copy-start | bytes 49156
  167.0 260.3 %copy-start.11 = (f32[4096]{0:T(1024)S(1)}, f32[4096]{0:T(1024)}, u32[]{:S(2)}) copy-start(f32[4096]{0:T(1024)} %param.12) | copy-start | bytes 49156
  434.7 3.4 copy-start.7
  582.6 296.5 %all-gather.13.cloned.1.call-start = ((), (), s32[]{:S(2)}) async-start(), calls=%async_computation.3 | async-start | bytes 17301504 | tf_op jit(solution)/shard_map/all_gather | solution.py:433
  582.8 10.5 copy-start.13
  741.0 233.5 %all-gather.15.cloned.1.call-start = ((), (), s32[]{:S(2)}) async-start(), calls=%async_computation.4 | async-start | bytes 8650752 | tf_op jit(solution)/shard_map/all_gather | solution.py:442
  758.4 2.0 copy-start.1
  879.1 196.9 %all-gather.17.cloned.1.call-start = ((), (), s32[]{:S(2)}) async-start(), calls=%async_computation.5 | async-start | bytes 8650752 | tf_op jit(solution)/shard_map/all_gather | solution.py:447
  879.2 2.2 copy-start.2
  988.1 5.8 copy-start.6
  1057.9 5.8 copy-start.3
  1063.7 8.7 copy-start.4
  1076.0 3.4 copy-start.5
Sparse Core Ops, SparseCore 0:
  147.1 99.0 all-gather.6
  249.6 278.6 all-gather.8
  582.7 156.2 all-gather.10
  741.7 137.3 all-gather.12
  881.8 92.2 all-gather.14
  976.9 74.9 all-gather.16

commit v4 on v3

--- a/solution.py
+++ b/solution.py
@@ -8,7 +8,7 @@
 from jax.sharding import PartitionSpec as P
 
 MESH = pl.DeviceIdType.MESH
-PARTS = 16
+PARTS = 8
 
 
 def spread_kernel(n, in_ref, out_ref, send_sem, recv_sem):
@@ -50,7 +50,7 @@
     )(block)
 
 
-def reduce_kernel(tile, steps, in_ref, out_ref, acc, *scratch):
+def reduce_kernel(tile, steps, in_ref, out_ref, fresh, held, *scratch):
     got, (load_sem, send_sem, recv_sem, store_sem) = scratch[:steps], scratch[steps:]
     me = lax.axis_index('dp')
     core = lax.rem(me, 2)
@@ -62,9 +62,7 @@
     turned = ((4, z0), (8, z1), one, two) if steps > 4 else ((4, z0), one, two)
 
     def way(part):
-        flip = 1 if isinstance(part, int) and part % 4 == 1 else 0
-        if not isinstance(part, int):
-            flip = (lax.rem(part, 4) + 3) // 4 * (1 - lax.rem(part, 4) // 2)
+        flip = (lax.rem(part, 4) + 3) // 4 * (1 - lax.rem(part, 4) // 2)
         return [(p + flip * (t - p), q + flip * (u - q)) for (p, q), (t, u) in zip(plain, turned)]
 
     def mate(step, part):
@@ -73,10 +71,9 @@
         weight, bit = way(part)[step - 1]
         return me + 2 * weight * (1 - 2 * bit)
 
-    mates = [mate(step, 0) for step in range(steps)]
     barrier = pltpu.get_barrier_semaphore()
-    for other in mates:
-        pl.semaphore_signal(barrier, inc=1, device_id=(other,), device_id_type=MESH)
+    for step in range(steps):
+        pl.semaphore_signal(barrier, inc=1, device_id=(mate(step, 0),), device_id_type=MESH)
 
     def piece(part):
         if tile[0] is None:
@@ -84,56 +81,52 @@
         return (pl.ds(pl.multiple_of(part * tile[0], tile[0]), tile[0]),)
 
     def load(part):
-        return pltpu.make_async_copy(in_ref.at[(slice(None), core) + piece(part)], acc.at[part], load_sem.at[part])
-
-    def begin(part, carry):
-        load(part).start()
-        return carry
-
-    lax.fori_loop(0, PARTS, begin, 0)
+        side = lax.rem(part, 2)
+        return pltpu.make_async_copy(in_ref.at[(slice(None), core) + piece(part)], fresh.at[side], load_sem.at[side])
+
+    load(0).start()
     pl.semaphore_wait(barrier, steps)
 
-    def place(step, part, i, theirs):
-        dims = way(part)
-        weight, bit = dims[step - 1]
-        at = weight * (1 - bit if theirs else bit)
-        for w, own in dims[:step - 1]:
-            at = at + w * own
-        for k, (w, _) in enumerate(dims[step:]):
-            at = at + w * lax.rem(i // 2 ** k, 2)
+    def start_of(step, part, theirs):
+        at = 0
+        for k, (_, own) in enumerate(way(part)[:step]):
+            bit = 1 - own if theirs and k == step - 1 else own
+            at = at + bit * (1 << (steps - 2 - k))
         return at
 
     def send(step, part):
         if step == 0:
-            pltpu.make_async_remote_copy(
-                src_ref=in_ref.at[(slice(None), 1 - core) + piece(part)], dst_ref=got[0].at[part],
-                send_sem=send_sem.at[0, part], recv_sem=recv_sem.at[0, part],
-                device_id=(mate(0, part),), device_id_type=MESH).start()
-            return
-
-        def one(i, carry):
-            pltpu.make_async_remote_copy(
-                src_ref=acc.at[part, place(step, part, i, True)], dst_ref=got[step].at[part, i],
-                send_sem=send_sem.at[step, part], recv_sem=recv_sem.at[step, part],
-                device_id=(mate(step, part),), device_id_type=MESH).start()
-            return carry
-        lax.fori_loop(0, got[step].shape[1], one, 0)
-
-    def whole(step, part):
+            source = in_ref.at[(slice(None), 1 - core) + piece(part)]
+        else:
+            source = held.at[part, pl.ds(start_of(step, part, True), got[step].shape[1])]
+        pltpu.make_async_remote_copy(
+            src_ref=source, dst_ref=got[step].at[part], send_sem=send_sem.at[step, part],
+            recv_sem=recv_sem.at[step, part], device_id=(mate(step, part),), device_id_type=MESH).start()
+
+    def landed(step, part):
         return pltpu.make_async_remote_copy(
             src_ref=got[step].at[part], dst_ref=got[step].at[part],
             send_sem=send_sem.at[step, part], recv_sem=recv_sem.at[step, part],
             device_id=(mate(step, part),), device_id_type=MESH)
 
     def add(step, part):
+        dims = way(part)
+        start = start_of(step, part, False)
+
         def one(i, carry):
-            at = i if step == 0 else place(step, part, i, False)
-            acc[part, at] = acc[part, at] + got[step][part, i]
+            if step == 0:
+                at = 0
+                for k, (weight, _) in enumerate(dims):
+                    at = at + lax.rem(i // weight, 2) * (1 << (steps - 2 - k))
+                held[part, at] = fresh[lax.rem(part, 2), i] + got[0][part, i]
+            else:
+                held[part, start + i] = held[part, start + i] + got[step][part, i]
             return carry
         lax.fori_loop(0, got[step].shape[1], one, 0)
 
     def store(part):
-        return pltpu.make_async_copy(acc.at[part, me // 2], out_ref.at[piece(part)], store_sem.at[part])
+        return pltpu.make_async_copy(held.at[part, start_of(steps - 1, part, False)], out_ref.at[piece(part)],
+                                     store_sem.at[part])
 
     def tick(t, carry):
         @pl.when(t < PARTS)
@@ -147,7 +140,11 @@
             def _():
                 if step == 0:
                     load(part).wait()
-                whole(step, part).wait_recv()
+
+                    @pl.when(part + 1 < PARTS)
+                    def _():
+                        load(part + 1).start()
+                landed(step, part).wait_recv()
                 add(step, part)
                 if step < steps - 1:
                     send(step + 1, part)
@@ -160,7 +157,7 @@
 
     def finish(part, carry):
         for step in range(steps):
-            whole(step, part).wait_send()
+            landed(step, part).wait_send()
         store(part).wait()
         return carry
 
@@ -181,14 +178,14 @@
         out_shape=jax.ShapeDtypeStruct((per,) + rest, x.dtype),
         in_specs=[pl.BlockSpec(memory_space=pl.ANY)],
         out_specs=pl.BlockSpec(memory_space=pl.ANY),
-        scratch_shapes=[pltpu.VMEM((PARTS, n // 2) + piece, x.dtype)] + got + [
-            pltpu.SemaphoreType.DMA((PARTS,)),
+        scratch_shapes=[pltpu.VMEM((2, n // 2) + piece, x.dtype), pltpu.VMEM((PARTS, n // 2) + piece, x.dtype)] + got + [
+            pltpu.SemaphoreType.DMA((2,)),
             pltpu.SemaphoreType.DMA((steps, PARTS)),
             pltpu.SemaphoreType.DMA((steps, PARTS)),
             pltpu.SemaphoreType.DMA((PARTS,)),
         ],
         compiler_params=pltpu.CompilerParams(collective_id=cid, has_side_effects=True,
-                                             vmem_limit_bytes=min(size * 3 // 2 + 4 * 2**20, 67043328)),
+                                             vmem_limit_bytes=min(size * 7 // 4 + 4 * 2**20, 67043328)),
         name=f'reduce_{cid}',
     )(x.reshape((n // 2, 2, per) + rest))
 
@@ -347,29 +344,6 @@
         compiler_params=pltpu.CompilerParams(vmem_limit_bytes=16 * 2**20), name='carry_over')(x)
 
 
-def fill_low(x):
-    rows, cols = x.shape
-    spec = pl.BlockSpec((rows // 4, cols), lambda i: (i, 0))
-    return pl.pallas_call(
-        carry_kernel, grid=(4,), out_shape=jax.ShapeDtypeStruct((2 * rows, cols), x.dtype), in_specs=[spec], out_specs=spec,
-        cost_estimate=pl.CostEstimate(flops=x.size, bytes_accessed=8 * x.size, transcendentals=0),
-        compiler_params=pltpu.CompilerParams(vmem_limit_bytes=16 * 2**20), name='fill_low')(x)
-
-
-def high_kernel(whole_ref, in_ref, out_ref):
-    out_ref[...] = in_ref[...]
-
-
-def fill_high(whole, x):
-    rows, cols = x.shape
-    return pl.pallas_call(
-        high_kernel, grid=(4,), out_shape=jax.ShapeDtypeStruct(whole.shape, x.dtype),
-        in_specs=[pl.BlockSpec(memory_space=pl.ANY), pl.BlockSpec((rows // 4, cols), lambda i: (i, 0))],
-        out_specs=pl.BlockSpec((rows // 4, cols), lambda i: (i + 4, 0)), input_output_aliases={0: 0},
-        cost_estimate=pl.CostEstimate(flops=x.size, bytes_accessed=8 * x.size, transcendentals=0),
-        compiler_params=pltpu.CompilerParams(vmem_limit_bytes=16 * 2**20), name='fill_high')(whole, x)
-
-
 def solution(mesh):
     n = mesh.shape['dp']
 
@@ -434,18 +408,11 @@
 
         d_act = jnp.einsum('td,fd->tf', d_query, w_two, preferred_element_type=jnp.float32)
         d_pre = gelu_back(d_act.astype(jnp.bfloat16).astype(jnp.float32))[0].astype(jnp.bfloat16)
-        half = x_flip.shape[0] // 2
-        low = outer(x_flip[:half], d_pre)
-        low, own_two = lax.optimization_barrier((low, own_two))
-        own_low = reduce_scatter(low, n, 3)
-        sent_low, grad_two = lax.optimization_barrier((own_low, grad_two))
-        all_low = lax.all_gather(sent_low, 'dp', tiled=True)
-        high = outer(x_flip[half:], d_pre)
-        high, own_low = lax.optimization_barrier((high, own_low))
-        own_high = reduce_scatter(high, n, 7)
-        sent_high, all_low = lax.optimization_barrier((own_high, all_low))
-        all_high = lax.all_gather(sent_high, 'dp', tiled=True)
-        grad_one = fill_high(fill_low(all_low), all_high)
+        part_one = outer(x_flip, d_pre)
+        part_one, own_two = lax.optimization_barrier((part_one, own_two))
+        own_one = reduce_scatter(part_one, n, 3)
+        sent_one, grad_two = lax.optimization_barrier((own_one, grad_two))
+        grad_one = carry_over(lax.all_gather(sent_one, 'dp', tiled=True))
         grad_two = carry_over(grad_two)
 
         grad_table = table_grad(keys, first, last, notes[:, :tok_dev].reshape(-1), query_all, cand_grad, rows_dev, n, count)

time: 1100 us -> 1040 us (0.945); the launches traced: 1090 us -> 1040 us
  Pallas kernels: 950 us -> 888 us
    pallas_call x6 -> x5, Pallas kernels: 797 us -> 733 us  [reduce_scatter(): pl.pallas_call(functools.partial(reduce_kernel, tile, steps), out_shape=j...]
    all_gather x2 -> x1, waiting for transfers between devices: 0.02 us -> 22.3 us  [local_step(): grad_one = carry_over(lax.all_gather(sent_one, 'dp', tiled=True))]
    all_gather x1, waiting for transfers between devices: 15.4 us -> 0.02 us  [local_step(): grad_two = lax.all_gather(sent_two, 'dp', tiled=True)]
    unnamed x37 -> x41, local copies, waits for them, and re-layouts: 38.5 us -> 40.8 us
  transfers between devices with their start and end apart: 6 -> 5, of which waited for: 1 -> 1; matrix products, arithmetic and copies ran while one was open for 6% -> 7% of each run, Pallas kernels for 75% -> 74%
where the time goes in v4:
time: 1040 us
  Pallas kernels  888 us (85%)
  matrix products  66.9 us (6%)
  local copies, waits for them, and re-layouts  43.4 us (4%)
  waiting for transfers between devices  22.5 us (2%)
  between operations  15.9 us (2%)
    pallas_call x5, Pallas kernels, reduce_scatter(): pl.pallas_call(functools.partial(reduce_kernel, tile, steps), out_shape=j...  733 us
    pallas_call x1, Pallas kernels, table_grad(): pl.pallas_call(functools.partial(table_kernel, n, count, tok_dev, rows_de...  66.8 us
    pallas_call x1, Pallas kernels, pick_rows(): pl.pallas_call(functools.partial(pick_kernel, n, count, table3.shape[0]),...  45.7 us
    unnamed x41, local copies, waits for them, and re-layouts  40.8 us
    pallas_call x2, Pallas kernels, spread(): pl.pallas_call(functools.partial(spread_kernel, n), out_shape=jax.ShapeDt...  22.7 us
    all_gather x1, waiting for transfers between devices, local_step(): grad_one = carry_over(lax.all_gather(sent_one, 'dp', tiled=True))  22.3 us
  transfers between devices with their start and end apart: 5, of which 1 were waited for; matrix products, arithmetic and copies ran while one was open for 7% of the time, Pallas kernels for 74%

profile of v4, /device:TPU:0, one launch (start us, length us, event | category | flops | bytes accessed | tf_op | source)
XLA Modules:
  0.0 1043.6 jit_solution(4079166049146687980)
XLA Ops:
  9.8 11.9 %spread_0.1 = s32[32,8,128]{2,1,0:T(8,128)} custom-call(s32[8,128]{1,0:T(8,128)} %pad_bitcast_fusion.1.in_ref), custom_call_target="tpu_custom_call" | custom-call | tf_op jit(solution)/shard_map/spread_0/pallas_call | solution.py:42
  22.9 8.9 copy.20
  35.2 45.7 %pick_rows.1 = (bf16[32,512,8,128]{3,2,1,0:T(8,128)(2,1)}, bf16[32,128,8,128]{3,2,1,0:T(8,128)(2,1)S(1)}) custom-call(s32[20480]{0:T(1024)S(1)} %reshape.97.keys, s32[32]{0:T(128)S(1)} %get-tuple-element.29.first, s32[32]{0:T(128)S(1)} %get-tuple-element.28.last, bf16[4096,8,128]{2,1,0:T(8,128)(2,1)S(1)} %bitcast.46), custom_call_target="tpu_custom_call" | custom-call | tf_op jit(solution)/shard_map/pick_rows/pallas_call | solution.py:245
  80.9 53.8 %reduce_5.1 = bf16[128,8,128]{2,1,0:T(8,128)(2,1)S(1)} custom-call(bf16[16,2,128,8,128]{4,3,2,1,0:T(8,128)(2,1)S(1)} %bitcast.49), custom_call_target="tpu_custom_call" | custom-call | tf_op jit(solution)/shard_map/reduce_5/pallas_call | solution.py:176
  135.5 8.2 convolution_convert_fusion.1
  143.7 10.2 convolution_convert_fusion.2
  155.5 237.6 %reduce_6.1 = bf16[512,8,128]{2,1,0:T(8,128)(2,1)} custom-call(bf16[16,2,512,8,128]{4,3,2,1,0:T(8,128)(2,1)} %bitcast.54), custom_call_target="tpu_custom_call" | custom-call | tf_op jit(solution)/shard_map/reduce_6/pallas_call | solution.py:176
  394.7 7.3 fusion.19
  404.5 8.7 fusion.18
  413.2 5.8 copy-done.3
  418.9 147.8 %reduce_1.1 = f32[128,1024]{1,0:T(8,128)S(1)} custom-call(f32[16,2,128,1024]{3,2,1,0:T(8,128)S(1)} %bitcast.47), custom_call_target="tpu_custom_call" | custom-call | tf_op jit(solution)/shard_map/reduce_1/pallas_call | solution.py:176
  568.0 10.5 %fusion.13 = bf16[512,1024]{1,0:T(8,128)(2,1)S(1)} fusion(bf16[4096,1024]{1,0:T(8,128)(2,1)} %all-gather.6.cloned.1.call-done, f32[512]{0:T(512)S(1)} %add_multiply_fusion.1, bf16[64,8,8,128]{3,2,1,0:T(8,128)(2,1)S(1)} %bitcast.57, f32[512,4096]{1,0:T(8,128)} %copy-done.6, f32[512]{0:T(512)S(1)} %get-tuple-element.31), kind=kOutput, calls=%fused_computation.26 | convolution fusion | flops 4303355904 | bytes 18878464 | tf_op jit(solution)/shard_map/dot_general | solution.py:393
  578.5 9.9 fusion.15
  588.4 5.8 copy-done.4
  594.1 139.6 %reduce_2.1 = f32[128,1024]{1,0:T(8,128)} custom-call(f32[16,2,128,1024]{3,2,1,0:T(8,128)S(1)} %bitcast.48), custom_call_target="tpu_custom_call" | custom-call | tf_op jit(solution)/shard_map/reduce_2/pallas_call | solution.py:176
  734.7 12.2 %fusion.3.right = bf16[512,4096]{1,0:T(8,128)(2,1)S(1)} fusion(bf16[512,4096]{1,0:T(8,128)(2,1)} %copy-done.12, bf16[512,1024]{1,0:T(8,128)(2,1)S(1)} %copy-done.15, bf16[4096,1024]{1,0:T(8,128)(2,1)} %param.9), kind=kOutput, calls=%fused_computation.9 | convolution fusion | flops 4343201792 | bytes 17825792 | tf_op jit(solution)/shard_map/td,fd->tf/dot_general | solution.py:409
  746.8 7.0 outer.1
  753.9 154.0 %reduce_3.1 = f32[32,4096]{1,0:T(8,128)} custom-call(f32[16,2,32,4096]{3,2,1,0:T(8,128)S(1)} %bitcast.45), custom_call_target="tpu_custom_call" | custom-call | tf_op jit(solution)/shard_map/reduce_3/pallas_call | solution.py:176
  909.2 10.8 %spread_4.1 = f32[32,8,128]{2,1,0:T(8,128)} custom-call(f32[8,128]{1,0:T(8,128)} %pad_bitcast_fusion.in_ref), custom_call_target="tpu_custom_call" | custom-call | tf_op jit(solution)/shard_map/spread_4/pallas_call | solution.py:42
  928.0 66.8 %table_grad.1 = f32[4096,1024]{1,0:T(8,128)} custom-call(s32[20480]{0:T(1024)S(1)} %reshape.97.keys, s32[32]{0:T(128)S(1)} %get-tuple-element.29.first, s32[32]{0:T(128)S(1)} %get-tuple-element.28.last, f32[16384]{0:T(1024)S(1)} %bitcast.53, bf16[16384,8,128]{2,1,0:T(8,128)(2,1)} %all-gather.8.cloned.1.call-done.query, f32[4096,8,128]{2,1,0:T(8,128)S(1)} %copy-done.5), custom_call_target="tpu_custom_call" | custom-call | flops 30000001024 | bytes 67108864 | tf_op jit(solution)/shard_map/table_grad/pallas_call | solution.py:299
  994.8 6.5 carry_over.3
  1001.3 22.3 %all-gather.14.cloned.1.call-done.in_ref = f32[1024,4096]{1,0:T(8,128)} async-done(((f32[32,4096]{1,0:T(8,128)}), f32[1024,4096]{1,0:T(8,128)}) %all-gather.14.cloned.1.call-update) | async-done | bytes 16777232 | tf_op jit(solution)/shard_map/all_gather | solution.py:415
  1023.6 5.8 copy-done.2
  1029.4 6.5 carry_over.2
  (65 shorter events, 24.1 us)
Async XLA Ops:
  7.2 387.5 %all-gather.6.cloned.1.call-start = ((), (), s32[]{:S(2)}) async-start(), calls=%async_computation | async-start | bytes 8650752 | tf_op jit(solution)/shard_map/all_gather | solution.py:372
  31.8 3.4 copy-start
  35.2 100.3 %copy-start.8 = (bf16[512,1024]{1,0:T(8,128)(2,1)S(1)}, bf16[512,1024]{1,0:T(8,128)(2,1)}, u32[]{:S(2)}) copy-start(bf16[512,1024]{1,0:T(8,128)(2,1)} %param.7) | copy-start | bytes 3145732
  135.4 432.2 %all-gather.8.cloned.1.call-start = ((), (), s32[]{:S(2)}) async-start(), calls=%async_computation.1 | async-start | bytes 34603008 | tf_op jit(solution)/shard_map/all_gather | solution.py:379
  143.7 10.3 copy-start.12
  155.2 578.5 %all-gather.10.cloned.1.call-start = ((), (), s32[]{:S(2)}) async-start(), calls=%async_computation.2 | async-start | bytes 17301504 | tf_op jit(solution)/shard_map/all_gather | solution.py:401
  155.5 239.2 %copy-start.9 = (s32[512]{0:T(512)S(1)}, s32[512]{0:T(512)}, u32[]{:S(2)}) copy-start(s32[512]{0:T(512)} %param.13) | copy-start | bytes 6148
  155.5 239.2 %copy-start.10 = (s32[4096]{0:T(1024)S(1)}, s32[4096]{0:T(1024)}, u32[]{:S(2)}) copy-start(s32[4096]{0:T(1024)} %param.11) | copy-start | bytes 49156
  155.5 239.2 %copy-start.11 = (f32[4096]{0:T(1024)S(1)}, f32[4096]{0:T(1024)}, u32[]{:S(2)}) copy-start(f32[4096]{0:T(1024)} %param.12) | copy-start | bytes 49156
  402.1 11.1 %copy-start.6 = (f32[512,4096]{1,0:T(8,128)}, f32[512,4096]{1,0:T(8,128)S(1)}, u32[]{:S(2)}) copy-start(f32[512,4096]{1,0:T(8,128)S(1)} %get-tuple-element.34) | copy-start | bytes 25165828
  413.2 5.8 copy-start.3
  418.9 149.1 %copy-start.7 = (bf16[512,8,128]{2,1,0:T(8,128)(2,1)S(1)}, bf16[512,8,128]{2,1,0:T(8,128)(2,1)}, u32[]{:S(2)}) copy-start(bf16[512,8,128]{2,1,0:T(8,128)(2,1)} %reduce_6.1) | copy-start | bytes 3145732
  567.7 340.2 %all-gather.12.cloned.1.call-start = ((), (), s32[]{:S(2)}) async-start(), calls=%async_computation.3 | async-start | bytes 17301504 | tf_op jit(solution)/shard_map/all_gather | solution.py:407
  568.0 10.5 %copy-start.13 = (bf16[512,4096]{1,0:T(8,128)(2,1)S(1)}, bf16[512,4096]{1,0:T(8,128)(2,1)}, u32[]{:S(2)}) copy-start(bf16[512,4096]{1,0:T(8,128)(2,1)} %copy-done.12) | copy-start | bytes 12582916
  578.5 9.9 copy-start.14
  588.4 5.8 copy-start.4
  594.1 140.5 %copy-start.15 = (bf16[512,1024]{1,0:T(8,128)(2,1)S(1)}, bf16[512,1024]{1,0:T(8,128)(2,1)}, u32[]{:S(2)}) copy-start(bf16[512,1024]{1,0:T(8,128)(2,1)} %copy-done.14) | copy-start | bytes 3145732
  733.8 289.8 %all-gather.14.cloned.1.call-start = ((), (), s32[]{:S(2)}) async-start(), calls=%async_computation.4 | async-start | bytes 17301504 | tf_op jit(solution)/shard_map/all_gather | solution.py:415
  922.2 5.8 copy-start.5
  928.0 66.8 %copy-start.1 = (f32[4096,1024]{1,0:T(8,128)S(1)}, f32[4096,1024]{1,0:T(8,128)}, u32[]{:S(2)}) copy-start(f32[4096,1024]{1,0:T(8,128)} %all-gather.12.cloned.1.call-done.in_ref) | copy-start | bytes 50331652
  1023.6 5.8 copy-start.2
Sparse Core Ops, SparseCore 0:
  135.6 108.8 all-gather.5
  247.4 286.2 all-gather.7
  567.8 158.5 all-gather.9
  733.9 158.6 all-gather.11
  908.1 115.4 all-gather.13

commit v5 on v4

--- a/solution.py
+++ b/solution.py
@@ -82,9 +82,10 @@
 
     def load(part):
         side = lax.rem(part, 2)
-        return pltpu.make_async_copy(in_ref.at[(slice(None), core) + piece(part)], fresh.at[side], load_sem.at[side])
+        return pltpu.make_async_copy(in_ref.at[(slice(None), slice(None)) + piece(part)], fresh.at[side], load_sem.at[side])
 
     load(0).start()
+    load(1).start()
     pl.semaphore_wait(barrier, steps)
 
     def start_of(step, part, theirs):
@@ -96,9 +97,15 @@
 
     def send(step, part):
         if step == 0:
-            source = in_ref.at[(slice(None), 1 - core) + piece(part)]
-        else:
-            source = held.at[part, pl.ds(start_of(step, part, True), got[step].shape[1])]
+            group = got[0].shape[1] // 4
+            for k in range(4):
+                run = pl.ds(k * group, group)
+                pltpu.make_async_remote_copy(
+                    src_ref=fresh.at[lax.rem(part, 2), run, 1 - core], dst_ref=got[0].at[part, run],
+                    send_sem=send_sem.at[0, part], recv_sem=recv_sem.at[0, part],
+                    device_id=(mate(0, part),), device_id_type=MESH).start()
+            return
+        source = held.at[part, pl.ds(start_of(step, part, True), got[step].shape[1])]
         pltpu.make_async_remote_copy(
             src_ref=source, dst_ref=got[step].at[part], send_sem=send_sem.at[step, part],
             recv_sem=recv_sem.at[step, part], device_id=(mate(step, part),), device_id_type=MESH).start()
@@ -118,7 +125,7 @@
                 at = 0
                 for k, (weight, _) in enumerate(dims):
                     at = at + lax.rem(i // weight, 2) * (1 << (steps - 2 - k))
-                held[part, at] = fresh[lax.rem(part, 2), i] + got[0][part, i]
+                held[part, at] = fresh[lax.rem(part, 2), i, core] + got[0][part, i]
             else:
                 held[part, start + i] = held[part, start + i] + got[step][part, i]
             return carry
@@ -131,6 +138,7 @@
     def tick(t, carry):
         @pl.when(t < PARTS)
         def _():
+            load(t).wait()
             send(0, t)
 
         for step in range(steps):
@@ -138,25 +146,25 @@
 
             @pl.when((part >= 0) & (part < PARTS))
             def _():
-                if step == 0:
-                    load(part).wait()
-
-                    @pl.when(part + 1 < PARTS)
-                    def _():
-                        load(part + 1).start()
                 landed(step, part).wait_recv()
                 add(step, part)
                 if step < steps - 1:
                     send(step + 1, part)
                 else:
                     store(part).start()
+                if step == 0:
+                    landed(0, part).wait_send()
+
+                    @pl.when(part + 2 < PARTS)
+                    def _():
+                        load(part + 2).start()
 
         return carry
 
     lax.fori_loop(0, PARTS + steps, tick, 0)
 
     def finish(part, carry):
-        for step in range(steps):
+        for step in range(1, steps):
             landed(step, part).wait_send()
         store(part).wait()
         return carry
@@ -178,14 +186,14 @@
         out_shape=jax.ShapeDtypeStruct((per,) + rest, x.dtype),
         in_specs=[pl.BlockSpec(memory_space=pl.ANY)],
         out_specs=pl.BlockSpec(memory_space=pl.ANY),
-        scratch_shapes=[pltpu.VMEM((2, n // 2) + piece, x.dtype), pltpu.VMEM((PARTS, n // 2) + piece, x.dtype)] + got + [
+        scratch_shapes=[pltpu.VMEM((2, n // 2, 2) + piece, x.dtype), pltpu.VMEM((PARTS, n // 2) + piece, x.dtype)] + got + [
             pltpu.SemaphoreType.DMA((2,)),
             pltpu.SemaphoreType.DMA((steps, PARTS)),
             pltpu.SemaphoreType.DMA((steps, PARTS)),
             pltpu.SemaphoreType.DMA((PARTS,)),
         ],
         compiler_params=pltpu.CompilerParams(collective_id=cid, has_side_effects=True,
-                                             vmem_limit_bytes=min(size * 7 // 4 + 4 * 2**20, 67043328)),
+                                             vmem_limit_bytes=min(size * 15 // 8 + 4 * 2**20, 67043328)),
         name=f'reduce_{cid}',
     )(x.reshape((n // 2, 2, per) + rest))
 

time: 1040 us -> 1030 us (level)
  Pallas kernels: 888 us -> 874 us
    pallas_call x5, Pallas kernels: 733 us -> 715 us  [reduce_scatter(): pl.pallas_call(functools.partial(reduce_kernel, tile, steps), out_shape=j...]
    unnamed x41 -> x49, local copies, waits for them, and re-layouts: 40.8 us -> 41.8 us
where the time goes in v5:
time: 1030 us
  Pallas kernels  874 us (85%)
  matrix products  67.3 us (7%)
  local copies, waits for them, and re-layouts  44.4 us (4%)
  waiting for transfers between devices  20 us (2%)
  between operations  15.9 us (2%)
    pallas_call x5, Pallas kernels, reduce_scatter(): pl.pallas_call(functools.partial(reduce_kernel, tile, steps), out_shape=j...  715 us
    pallas_call x1, Pallas kernels, table_grad(): pl.pallas_call(functools.partial(table_kernel, n, count, tok_dev, rows_de...  68.1 us
    pallas_call x1, Pallas kernels, pick_rows(): pl.pallas_call(functools.partial(pick_kernel, n, count, table3.shape[0]),...  46.6 us
    unnamed x49, local copies, waits for them, and re-layouts  41.8 us
    pallas_call x2, Pallas kernels, spread(): pl.pallas_call(functools.partial(spread_kernel, n), out_shape=jax.ShapeDt...  23.8 us
  transfers between devices with their start and end apart: 5, of which 1 were waited for; matrix products, arithmetic and copies ran while one was open for 7% of the time, Pallas kernels for 74%

profile of v5, /device:TPU:0, one launch (start us, length us, event | category | flops | bytes accessed | tf_op | source)
XLA Modules:
  0.0 1028.7 jit_solution(5879412545039731141)
XLA Ops:
  9.8 11.9 %spread_0.1 = s32[32,8,128]{2,1,0:T(8,128)} custom-call(s32[8,128]{1,0:T(8,128)} %pad_bitcast_fusion.1.in_ref), custom_call_target="tpu_custom_call" | custom-call | tf_op jit(solution)/shard_map/spread_0/pallas_call | solution.py:42
  22.9 9.0 copy.20
  35.3 46.6 %pick_rows.1 = (bf16[32,512,8,128]{3,2,1,0:T(8,128)(2,1)}, bf16[32,128,8,128]{3,2,1,0:T(8,128)(2,1)S(1)}) custom-call(s32[20480]{0:T(1024)S(1)} %reshape.97.keys, s32[32]{0:T(128)S(1)} %get-tuple-element.29.first, s32[32]{0:T(128)S(1)} %get-tuple-element.28.last, bf16[4096,8,128]{2,1,0:T(8,128)(2,1)S(1)} %bitcast.46), custom_call_target="tpu_custom_call" | custom-call | tf_op jit(solution)/shard_map/pick_rows/pallas_call | solution.py:253
  81.9 51.6 %reduce_5.1 = bf16[128,8,128]{2,1,0:T(8,128)(2,1)S(1)} custom-call(bf16[16,2,128,8,128]{4,3,2,1,0:T(8,128)(2,1)S(1)} %bitcast.49), custom_call_target="tpu_custom_call" | custom-call | tf_op jit(solution)/shard_map/reduce_5/pallas_call | solution.py:184
  134.3 8.1 convolution_convert_fusion.1
  142.5 10.3 convolution_convert_fusion.2
  155.2 235.7 %reduce_6.1 = bf16[512,8,128]{2,1,0:T(8,128)(2,1)} custom-call(bf16[16,2,512,8,128]{4,3,2,1,0:T(8,128)(2,1)} %bitcast.54), custom_call_target="tpu_custom_call" | custom-call | tf_op jit(solution)/shard_map/reduce_6/pallas_call | solution.py:184
  392.8 7.7 fusion.19
  403.0 8.7 fusion.18
  411.7 5.8 copy-done.3
  417.4 143.3 %reduce_1.1 = f32[128,1024]{1,0:T(8,128)S(1)} custom-call(f32[16,2,128,1024]{3,2,1,0:T(8,128)S(1)} %bitcast.47), custom_call_target="tpu_custom_call" | custom-call | tf_op jit(solution)/shard_map/reduce_1/pallas_call | solution.py:184
  562.0 10.5 %fusion.13 = bf16[512,1024]{1,0:T(8,128)(2,1)S(1)} fusion(bf16[4096,1024]{1,0:T(8,128)(2,1)} %all-gather.6.cloned.1.call-done, f32[512]{0:T(512)S(1)} %add_multiply_fusion.1, bf16[64,8,8,128]{3,2,1,0:T(8,128)(2,1)S(1)} %bitcast.57, f32[512,4096]{1,0:T(8,128)} %copy-done.12, f32[512]{0:T(512)S(1)} %get-tuple-element.31), kind=kOutput, calls=%fused_computation.26 | convolution fusion | flops 4303355904 | bytes 18878464 | tf_op jit(solution)/shard_map/dot_general | solution.py:401
  572.5 9.8 fusion.15
  582.3 5.8 copy-done.4
  588.1 139.2 %reduce_2.1 = f32[128,1024]{1,0:T(8,128)} custom-call(f32[16,2,128,1024]{3,2,1,0:T(8,128)S(1)} %bitcast.48), custom_call_target="tpu_custom_call" | custom-call | tf_op jit(solution)/shard_map/reduce_2/pallas_call | solution.py:184
  728.2 12.2 %fusion.3.right = bf16[512,4096]{1,0:T(8,128)(2,1)S(1)} fusion(bf16[512,4096]{1,0:T(8,128)(2,1)} %copy-done.18, bf16[512,1024]{1,0:T(8,128)(2,1)S(1)} %fusion.13, bf16[4096,1024]{1,0:T(8,128)(2,1)} %param.9), kind=kOutput, calls=%fused_computation.9 | convolution fusion | flops 4343201792 | bytes 17825792 | tf_op jit(solution)/shard_map/td,fd->tf/dot_general | solution.py:417
  740.3 7.0 outer.1
  747.4 145.6 %reduce_3.1 = f32[32,4096]{1,0:T(8,128)} custom-call(f32[16,2,32,4096]{3,2,1,0:T(8,128)S(1)} %bitcast.45), custom_call_target="tpu_custom_call" | custom-call | tf_op jit(solution)/shard_map/reduce_3/pallas_call | solution.py:184
  894.4 11.9 %spread_4.1 = f32[32,8,128]{2,1,0:T(8,128)} custom-call(f32[8,128]{1,0:T(8,128)} %pad_bitcast_fusion.in_ref), custom_call_target="tpu_custom_call" | custom-call | tf_op jit(solution)/shard_map/spread_4/pallas_call | solution.py:42
  914.3 68.1 %table_grad.1 = f32[4096,1024]{1,0:T(8,128)} custom-call(s32[20480]{0:T(1024)S(1)} %copy-done.6, s32[32]{0:T(128)S(1)} %copy-done.10, s32[32]{0:T(128)S(1)} %copy-done.8, f32[16384]{0:T(1024)S(1)} %bitcast.53, bf16[16384,8,128]{2,1,0:T(8,128)(2,1)} %all-gather.8.cloned.1.call-done.query, f32[4096,8,128]{2,1,0:T(8,128)S(1)} %copy-done.11), custom_call_target="tpu_custom_call" | custom-call | flops 30000001024 | bytes 67108864 | tf_op jit(solution)/shard_map/table_grad/pallas_call | solution.py:307
  982.4 6.5 carry_over.3
  988.9 19.9 %all-gather.14.cloned.1.call-done.in_ref = f32[1024,4096]{1,0:T(8,128)} async-done(((f32[32,4096]{1,0:T(8,128)}), f32[1024,4096]{1,0:T(8,128)}) %all-gather.14.cloned.1.call-update) | async-done | bytes 16777232 | tf_op jit(solution)/shard_map/all_gather | solution.py:423
  1008.8 5.8 copy-done.2
  1014.6 6.5 carry_over.2
  (73 shorter events, 25.4 us)
Async XLA Ops:
  7.2 385.6 %all-gather.6.cloned.1.call-start = ((), (), s32[]{:S(2)}) async-start(), calls=%async_computation | async-start | bytes 8650752 | tf_op jit(solution)/shard_map/all_gather | solution.py:380
  22.8 9.0 copy-start.7
  22.9 9.0 copy-start.9
  22.9 9.0 copy-start.5
  31.9 3.4 copy-start
  35.3 99.0 %copy-start.16 = (bf16[512,1024]{1,0:T(8,128)(2,1)S(1)}, bf16[512,1024]{1,0:T(8,128)(2,1)}, u32[]{:S(2)}) copy-start(bf16[512,1024]{1,0:T(8,128)(2,1)} %param.7) | copy-start | bytes 3145732
  134.3 427.4 %all-gather.8.cloned.1.call-start = ((), (), s32[]{:S(2)}) async-start(), calls=%async_computation.1 | async-start | bytes 34603008 | tf_op jit(solution)/shard_map/all_gather | solution.py:387
  142.4 10.3 %copy-start.18 = (bf16[512,4096]{1,0:T(8,128)(2,1)}, bf16[512,4096]{1,0:T(8,128)(2,1)S(1)}, u32[]{:S(2)}) copy-start(bf16[512,4096]{1,0:T(8,128)(2,1)S(1)} %convolution_convert_fusion.1) | copy-start | bytes 12582916
  155.0 572.3 %all-gather.10.cloned.1.call-start = ((), (), s32[]{:S(2)}) async-start(), calls=%async_computation.2 | async-start | bytes 17301504 | tf_op jit(solution)/shard_map/all_gather | solution.py:409
  400.5 11.1 %copy-start.12 = (f32[512,4096]{1,0:T(8,128)}, f32[512,4096]{1,0:T(8,128)S(1)}, u32[]{:S(2)}) copy-start(f32[512,4096]{1,0:T(8,128)S(1)} %get-tuple-element.34) | copy-start | bytes 25165828
  400.5 2.4 copy-start.15
  411.7 5.8 copy-start.3
  417.4 144.5 %copy-start.13 = (bf16[512,8,128]{2,1,0:T(8,128)(2,1)S(1)}, bf16[512,8,128]{2,1,0:T(8,128)(2,1)}, u32[]{:S(2)}) copy-start(bf16[512,8,128]{2,1,0:T(8,128)(2,1)} %reduce_6.1) | copy-start | bytes 3145732
  561.7 331.4 %all-gather.12.cloned.1.call-start = ((), (), s32[]{:S(2)}) async-start(), calls=%async_computation.3 | async-start | bytes 17301504 | tf_op jit(solution)/shard_map/all_gather | solution.py:415
  562.0 10.5 %copy-start.19 = (bf16[512,4096]{1,0:T(8,128)(2,1)S(1)}, bf16[512,4096]{1,0:T(8,128)(2,1)}, u32[]{:S(2)}) copy-start(bf16[512,4096]{1,0:T(8,128)(2,1)} %copy-done.18) | copy-start | bytes 12582916
  582.3 5.8 copy-start.4
  588.1 139.5 %copy-start.17 = (bf16[512,1024]{1,0:T(8,128)(2,1)S(1)}, bf16[512,1024]{1,0:T(8,128)(2,1)}, u32[]{:S(2)}) copy-start(bf16[512,1024]{1,0:T(8,128)(2,1)} %param.7) | copy-start | bytes 3145732
  727.3 281.5 %all-gather.14.cloned.1.call-start = ((), (), s32[]{:S(2)}) async-start(), calls=%async_computation.4 | async-start | bytes 17301504 | tf_op jit(solution)/shard_map/all_gather | solution.py:423
  747.4 161.1 %copy-start.6 = (s32[20480]{0:T(1024)S(1)}, s32[20480]{0:T(1024)}, u32[]{:S(2)}) copy-start(s32[20480]{0:T(1024)} %copy-done.5) | copy-start | bytes 245764
  747.4 161.1 %copy-start.8 = (s32[32]{0:T(128)S(1)}, s32[32]{0:T(128)}, u32[]{:S(2)}) copy-start(s32[32]{0:T(128)} %copy-done.7) | copy-start | bytes 388
  747.4 161.1 %copy-start.10 = (s32[32]{0:T(128)S(1)}, s32[32]{0:T(128)}, u32[]{:S(2)}) copy-start(s32[32]{0:T(128)} %copy-done.9) | copy-start | bytes 388
  908.5 5.8 copy-start.11
  914.3 68.1 %copy-start.1 = (f32[4096,1024]{1,0:T(8,128)S(1)}, f32[4096,1024]{1,0:T(8,128)}, u32[]{:S(2)}) copy-start(f32[4096,1024]{1,0:T(8,128)} %all-gather.12.cloned.1.call-done.in_ref) | copy-start | bytes 50331652
  1008.8 5.8 copy-start.2
  (1 other events, 1.0 us)
Sparse Core Ops, SparseCore 0:
  134.4 106.1 all-gather.5
  243.4 286.7 all-gather.7
  561.8 154.8 all-gather.9
  727.4 158.3 all-gather.11
  893.2 115.5 all-gather.13

commit v6 on v5

--- a/solution.py
+++ b/solution.py
@@ -56,12 +56,12 @@
     core = lax.rem(me, 2)
     xb, yb = lax.rem(me // 2, 2), lax.rem(me // 4, 2)
     z0, z1 = lax.rem(me // 8, 2), lax.rem(me // 16, 2)
-    one = (1 + core, xb * (1 - core) + yb * core)
-    two = (2 - core, yb * (1 - core) + xb * core)
-    plain = (one, two, (4, z0), (8, z1))[:steps - 1]
-    turned = ((4, z0), (8, z1), one, two) if steps > 4 else ((4, z0), one, two)
-
     def way(part):
+        turn = lax.rem(part - (part + 2) // 4 + core, 2)
+        one = (1 + turn, xb * (1 - turn) + yb * turn)
+        two = (2 - turn, yb * (1 - turn) + xb * turn)
+        plain = (one, two, (4, z0), (8, z1))[:steps - 1]
+        turned = ((4, z0), (8, z1), one, two) if steps > 4 else ((4, z0), one, two)
         flip = (lax.rem(part, 4) + 3) // 4 * (1 - lax.rem(part, 4) // 2)
         return [(p + flip * (t - p), q + flip * (u - q)) for (p, q), (t, u) in zip(plain, turned)]
 

time: 1030 us -> 1040 us (level)
    pallas_call x5, Pallas kernels: 715 us -> 728 us  [reduce_scatter(): pl.pallas_call(functools.partial(reduce_kernel, tile, steps), out_shape=j...]
  transfers between devices with their start and end apart: 5 -> 5, of which waited for: 1 -> 1; matrix products, arithmetic and copies ran while one was open for 7% -> 7% of each run, Pallas kernels for 74% -> 73%
where the time goes in v6:
time: 1040 us
  Pallas kernels  884 us (85%)
  matrix products  67.3 us (6%)
  local copies, waits for them, and re-layouts  44.4 us (4%)
  waiting for transfers between devices  22.4 us (2%)
  between operations  15.9 us (2%)
    pallas_call x5, Pallas kernels, reduce_scatter(): pl.pallas_call(functools.partial(reduce_kernel, tile, steps), out_shape=j...  728 us
    pallas_call x1, Pallas kernels, table_grad(): pl.pallas_call(functools.partial(table_kernel, n, count, tok_dev, rows_de...  66 us
    pallas_call x1, Pallas kernels, pick_rows(): pl.pallas_call(functools.partial(pick_kernel, n, count, table3.shape[0]),...  44.6 us
    unnamed x49, local copies, waits for them, and re-layouts  41.8 us
    pallas_call x2, Pallas kernels, spread(): pl.pallas_call(functools.partial(spread_kernel, n), out_shape=jax.ShapeDt...  25.9 us
    all_gather x1, waiting for transfers between devices, local_step(): grad_one = carry_over(lax.all_gather(sent_one, 'dp', tiled=True))  22.2 us
  transfers between devices with their start and end apart: 5, of which 1 were waited for; matrix products, arithmetic and copies ran while one was open for 7% of the time, Pallas kernels for 73%

profile of v6, /device:TPU:0, one launch (start us, length us, event | category | flops | bytes accessed | tf_op | source)
XLA Modules:
  0.0 1041.3 jit_solution(15526682900285245086)
XLA Ops:
  9.8 11.9 %spread_0.1 = s32[32,8,128]{2,1,0:T(8,128)} custom-call(s32[8,128]{1,0:T(8,128)} %pad_bitcast_fusion.1.in_ref), custom_call_target="tpu_custom_call" | custom-call | tf_op jit(solution)/shard_map/spread_0/pallas_call | solution.py:42
  22.9 9.0 copy.20
  35.3 44.6 %pick_rows.1 = (bf16[32,512,8,128]{3,2,1,0:T(8,128)(2,1)}, bf16[32,128,8,128]{3,2,1,0:T(8,128)(2,1)S(1)}) custom-call(s32[20480]{0:T(1024)S(1)} %reshape.97.keys, s32[32]{0:T(128)S(1)} %get-tuple-element.29.first, s32[32]{0:T(128)S(1)} %get-tuple-element.28.last, bf16[4096,8,128]{2,1,0:T(8,128)(2,1)S(1)} %bitcast.46), custom_call_target="tpu_custom_call" | custom-call | tf_op jit(solution)/shard_map/pick_rows/pallas_call | solution.py:253
  79.9 57.2 %reduce_5.1 = bf16[128,8,128]{2,1,0:T(8,128)(2,1)S(1)} custom-call(bf16[16,2,128,8,128]{4,3,2,1,0:T(8,128)(2,1)S(1)} %bitcast.49), custom_call_target="tpu_custom_call" | custom-call | tf_op jit(solution)/shard_map/reduce_5/pallas_call | solution.py:184
  137.9 8.1 convolution_convert_fusion.1
  146.0 10.3 convolution_convert_fusion.2
  158.8 233.2 %reduce_6.1 = bf16[512,8,128]{2,1,0:T(8,128)(2,1)} custom-call(bf16[16,2,512,8,128]{4,3,2,1,0:T(8,128)(2,1)} %bitcast.54), custom_call_target="tpu_custom_call" | custom-call | tf_op jit(solution)/shard_map/reduce_6/pallas_call | solution.py:184
  393.9 7.7 fusion.19
  404.1 8.7 fusion.18
  412.8 5.8 copy-done.3
  418.6 142.2 %reduce_1.1 = f32[128,1024]{1,0:T(8,128)S(1)} custom-call(f32[16,2,128,1024]{3,2,1,0:T(8,128)S(1)} %bitcast.47), custom_call_target="tpu_custom_call" | custom-call | tf_op jit(solution)/shard_map/reduce_1/pallas_call | solution.py:184
  562.0 10.5 %fusion.13 = bf16[512,1024]{1,0:T(8,128)(2,1)S(1)} fusion(bf16[4096,1024]{1,0:T(8,128)(2,1)} %all-gather.6.cloned.1.call-done, f32[512]{0:T(512)S(1)} %add_multiply_fusion.1, bf16[64,8,8,128]{3,2,1,0:T(8,128)(2,1)S(1)} %bitcast.57, f32[512,4096]{1,0:T(8,128)} %copy-done.12, f32[512]{0:T(512)S(1)} %get-tuple-element.31), kind=kOutput, calls=%fused_computation.26 | convolution fusion | flops 4303355904 | bytes 18878464 | tf_op jit(solution)/shard_map/dot_general | solution.py:401
  572.5 9.8 fusion.15
  582.4 5.8 copy-done.4
  588.1 146.6 %reduce_2.1 = f32[128,1024]{1,0:T(8,128)} custom-call(f32[16,2,128,1024]{3,2,1,0:T(8,128)S(1)} %bitcast.48), custom_call_target="tpu_custom_call" | custom-call | tf_op jit(solution)/shard_map/reduce_2/pallas_call | solution.py:184
  735.7 12.2 %fusion.3.right = bf16[512,4096]{1,0:T(8,128)(2,1)S(1)} fusion(bf16[512,4096]{1,0:T(8,128)(2,1)} %copy-done.18, bf16[512,1024]{1,0:T(8,128)(2,1)S(1)} %fusion.13, bf16[4096,1024]{1,0:T(8,128)(2,1)} %param.9), kind=kOutput, calls=%fused_computation.9 | convolution fusion | flops 4343201792 | bytes 17825792 | tf_op jit(solution)/shard_map/td,fd->tf/dot_general | solution.py:417
  747.8 7.0 outer.1
  754.9 148.4 %reduce_3.1 = f32[32,4096]{1,0:T(8,128)} custom-call(f32[16,2,32,4096]{3,2,1,0:T(8,128)S(1)} %bitcast.45), custom_call_target="tpu_custom_call" | custom-call | tf_op jit(solution)/shard_map/reduce_3/pallas_call | solution.py:184
  904.6 14.0 %spread_4.1 = f32[32,8,128]{2,1,0:T(8,128)} custom-call(f32[8,128]{1,0:T(8,128)} %pad_bitcast_fusion.in_ref), custom_call_target="tpu_custom_call" | custom-call | tf_op jit(solution)/shard_map/spread_4/pallas_call | solution.py:42
  926.6 66.0 %table_grad.1 = f32[4096,1024]{1,0:T(8,128)} custom-call(s32[20480]{0:T(1024)S(1)} %copy-done.6, s32[32]{0:T(128)S(1)} %copy-done.10, s32[32]{0:T(128)S(1)} %copy-done.8, f32[16384]{0:T(1024)S(1)} %bitcast.53, bf16[16384,8,128]{2,1,0:T(8,128)(2,1)} %all-gather.8.cloned.1.call-done.query, f32[4096,8,128]{2,1,0:T(8,128)S(1)} %copy-done.11), custom_call_target="tpu_custom_call" | custom-call | flops 30000001024 | bytes 67108864 | tf_op jit(solution)/shard_map/table_grad/pallas_call | solution.py:307
  992.7 6.5 carry_over.3
  999.2 22.2 %all-gather.14.cloned.1.call-done.in_ref = f32[1024,4096]{1,0:T(8,128)} async-done(((f32[32,4096]{1,0:T(8,128)}), f32[1024,4096]{1,0:T(8,128)}) %all-gather.14.cloned.1.call-update) | async-done | bytes 16777232 | tf_op jit(solution)/shard_map/all_gather | solution.py:423
  1021.4 5.8 copy-done.2
  1027.2 6.5 carry_over.2
  (73 shorter events, 25.4 us)
Async XLA Ops:
  7.2 386.8 %all-gather.6.cloned.1.call-start = ((), (), s32[]{:S(2)}) async-start(), calls=%async_computation | async-start | bytes 8650752 | tf_op jit(solution)/shard_map/all_gather | solution.py:380
  22.8 9.0 copy-start.7
  22.9 9.0 copy-start.9
  22.9 9.0 copy-start.5
  31.9 3.4 copy-start
  35.3 102.6 %copy-start.16 = (bf16[512,1024]{1,0:T(8,128)(2,1)S(1)}, bf16[512,1024]{1,0:T(8,128)(2,1)}, u32[]{:S(2)}) copy-start(bf16[512,1024]{1,0:T(8,128)(2,1)} %param.7) | copy-start | bytes 3145732
  137.8 423.9 %all-gather.8.cloned.1.call-start = ((), (), s32[]{:S(2)}) async-start(), calls=%async_computation.1 | async-start | bytes 34603008 | tf_op jit(solution)/shard_map/all_gather | solution.py:387
  146.0 10.3 copy-start.18
  158.5 576.2 %all-gather.10.cloned.1.call-start = ((), (), s32[]{:S(2)}) async-start(), calls=%async_computation.2 | async-start | bytes 17301504 | tf_op jit(solution)/shard_map/all_gather | solution.py:409
  401.7 11.1 %copy-start.12 = (f32[512,4096]{1,0:T(8,128)}, f32[512,4096]{1,0:T(8,128)S(1)}, u32[]{:S(2)}) copy-start(f32[512,4096]{1,0:T(8,128)S(1)} %get-tuple-element.34) | copy-start | bytes 25165828
  401.7 2.4 copy-start.15
  412.8 5.8 copy-start.3
  418.6 143.5 %copy-start.13 = (bf16[512,8,128]{2,1,0:T(8,128)(2,1)S(1)}, bf16[512,8,128]{2,1,0:T(8,128)(2,1)}, u32[]{:S(2)}) copy-start(bf16[512,8,128]{2,1,0:T(8,128)(2,1)} %reduce_6.1) | copy-start | bytes 3145732
  561.7 341.6 %all-gather.12.cloned.1.call-start = ((), (), s32[]{:S(2)}) async-start(), calls=%async_computation.3 | async-start | bytes 17301504 | tf_op jit(solution)/shard_map/all_gather | solution.py:415
  562.0 10.5 %copy-start.19 = (bf16[512,4096]{1,0:T(8,128)(2,1)S(1)}, bf16[512,4096]{1,0:T(8,128)(2,1)}, u32[]{:S(2)}) copy-start(bf16[512,4096]{1,0:T(8,128)(2,1)} %copy-done.18) | copy-start | bytes 12582916
  582.4 5.8 copy-start.4
  588.1 147.0 %copy-start.17 = (bf16[512,1024]{1,0:T(8,128)(2,1)S(1)}, bf16[512,1024]{1,0:T(8,128)(2,1)}, u32[]{:S(2)}) copy-start(bf16[512,1024]{1,0:T(8,128)(2,1)} %param.7) | copy-start | bytes 3145732
  734.8 286.6 %all-gather.14.cloned.1.call-start = ((), (), s32[]{:S(2)}) async-start(), calls=%async_computation.4 | async-start | bytes 17301504 | tf_op jit(solution)/shard_map/all_gather | solution.py:423
  754.9 165.9 %copy-start.6 = (s32[20480]{0:T(1024)S(1)}, s32[20480]{0:T(1024)}, u32[]{:S(2)}) copy-start(s32[20480]{0:T(1024)} %copy-done.5) | copy-start | bytes 245764
  754.9 165.9 %copy-start.8 = (s32[32]{0:T(128)S(1)}, s32[32]{0:T(128)}, u32[]{:S(2)}) copy-start(s32[32]{0:T(128)} %copy-done.7) | copy-start | bytes 388
  754.9 165.9 %copy-start.10 = (s32[32]{0:T(128)S(1)}, s32[32]{0:T(128)}, u32[]{:S(2)}) copy-start(s32[32]{0:T(128)} %copy-done.9) | copy-start | bytes 388
  920.9 5.8 copy-start.11
  926.6 66.0 %copy-start.1 = (f32[4096,1024]{1,0:T(8,128)S(1)}, f32[4096,1024]{1,0:T(8,128)}, u32[]{:S(2)}) copy-start(f32[4096,1024]{1,0:T(8,128)} %all-gather.12.cloned.1.call-done.in_ref) | copy-start | bytes 50331652
  1021.4 5.8 copy-start.2
  (1 other events, 1.0 us)
Sparse Core Ops, SparseCore 0:
  137.9 103.6 all-gather.5
  244.5 279.6 all-gather.7
  561.9 155.9 all-gather.9
  734.9 155.3 all-gather.11
  903.5 117.8 all-gather.13
